TPU v7x, 32 devices: a whole 2x2x4 slice. The times are simulated.
32 devices in a mesh: gx: 4 (over x, core), gy: 2 (over y), gz: 4 (over z).
Axes of the slice: x: 2, y: 2, z: 4, core: 2. Of those that a mesh axis runs over, the one named last changes fastest.
Arguments:
- warped_image: float32 [256, 128, 512], P('gx', 'gy', 'gz'), may hold values from -6 to 6
- fixed_image: float32 [256, 128, 512], P('gx', 'gy', 'gz'), may hold values from -6 to 6
- fine_control: float32 [3, 32, 16, 64], P(None, 'gx', 'gy', 'gz'), may hold values from -6 to 6
- coarse_control: float32 [3, 8, 4, 16], replicated, may hold values from -6 to 6
Outputs:
- fine_gradient: float32 [3, 32, 16, 64], P(None, 'gx', 'gy', 'gz')
- coarse_gradient: float32 [3, 8, 4, 16], replicated
All inputs are finite; a program needn't handle non-finite values.
Results may differ from a plain program's by a relative error of at most 0.0003.
Values sent between devices are 32-bit elements; how exact they have to be, the bound alone decides.
A program may use at most 64 MiB of HBM per device.

v0:
```python
import functools

import jax
import jax.numpy as jnp
from jax import lax
from jax.experimental import pallas as pl
from jax.experimental.pallas import tpu as pltpu
from jax.sharding import PartitionSpec as P

SPF = 8
SPC = 32
BEND = 0.01
HI = lax.Precision.HIGHEST
MESH = pl.DeviceIdType.MESH
f32 = jnp.float32
bf16 = jnp.bfloat16


def nn(a, b):
    return lax.dot_general(
        a, b, (((1,), (0,)), ((), ())), precision=HI, preferred_element_type=f32
    )


def nt(a, b):
    return lax.dot_general(
        a, b, (((1,), (1,)), ((), ())), precision=HI, preferred_element_type=f32
    )


def spline(t):
    m = jnp.abs(t)
    inner = 2.0 / 3.0 - m * m + 0.5 * m * m * m
    r = 2.0 - m
    outer = r * r * r * (1.0 / 6.0)
    return jnp.where(m < 1.0, inner, jnp.where(m < 2.0, outer, 0.0))


def weight(voxel, point, spacing):
    scaled = (2 * voxel + 1 - spacing * (2 * point + 1)).astype(f32)
    return spline(scaled * (0.5 / spacing))


def iota(shape, axis):
    return lax.broadcasted_iota(jnp.int32, shape, axis)


def diff1(out, inp):
    d = jnp.abs(out - inp)
    return jnp.where(d == 0, -2.0, jnp.where(d == 1, 1.0, 0.0)).astype(f32)


def diff2(out, inp, count):
    d = jnp.abs(out - inp)
    edge = (inp == 0) | (inp == count - 1)
    centre = jnp.where(edge, 5.0, 6.0)
    return jnp.where(
        d == 0, centre, jnp.where(d == 1, -4.0, jnp.where(d == 2, 1.0, 0.0))
    ).astype(f32)


def same(out, inp):
    return jnp.where(out == inp, 1.0, 0.0).astype(f32)


def bend_planes(px, py, qx, qy, cx, cy):
    jx, jy = same(px, qx), same(py, qy)
    tx, ty = diff1(px, qx), diff1(py, qy)
    m0 = diff2(px, qx, cx) * jy + jx * diff2(py, qy, cy) + 2.0 * tx * ty
    m1 = 2.0 * (tx * jy + jx * ty)
    return m0 * BEND, m1 * BEND, jx * jy * BEND


def kernel(sizes, w_hbm, f_hbm, fc_hbm, cc_hbm, fo_ref, co_ref,
           w_v, f_v, fc_ref, cc_ref, s_v, ysend, yrecv, zsend, zrecv, zcorr,
           wf_v, wc_v, fh_v, fl_v,
           accf, accc, tz_v, bend_v, ccp, bendc, zmsg, zgot, a_v, agot, b_v, bgot,
           cslots, load_sem, small_sem, hs_sem, hr_sem, ys_sem, yr_sem,
           ms_sem, mr_sem, cs_sem, cr_sem):
    nx, ny, nz = sizes
    axes = ("gx", "gy", "gz")
    counts = sizes
    me = [lax.axis_index(a) for a in axes]
    SX, SY, SZ = w_v.shape
    PX, PY, PZ = SX // SPF, SY // SPF, SZ // SPF
    KX, KY, KZ = cc_ref.shape[1:]
    EX, QE, QC = PX + 4, 2 * PY, accc.shape[1]
    cells = SX // SPF
    lanes = 3 * SZ

    loads = []
    for c in range(cells):
        part = pl.ds(c * SPF, SPF)
        loads.append((
            pltpu.make_async_copy(w_hbm.at[part], w_v.at[part], load_sem.at[0, c]),
            pltpu.make_async_copy(f_hbm.at[part], f_v.at[part], load_sem.at[1, c]),
        ))
    small = (pltpu.make_async_copy(fc_hbm, fc_ref, small_sem.at[0]),
             pltpu.make_async_copy(cc_hbm, cc_ref, small_sem.at[1]))
    order = [0, cells - 1] + list(range(1, cells - 1))
    for c in order:
        loads[c][0].start()
        loads[c][1].start()
    for copy in small:
        copy.start()

    zero_plane = jnp.zeros((2, SY, SZ), f32)
    s_v[0:2, 8:8 + SY, :] = zero_plane
    s_v[SX + 2:SX + 4, 8:8 + SY, :] = zero_plane
    yrecv[...] = jnp.zeros(yrecv.shape, f32)
    zrecv[...] = jnp.zeros(zrecv.shape, f32)
    zgot[...] = jnp.zeros(zgot.shape, f32)
    agot[...] = jnp.zeros(agot.shape, f32)
    bgot[...] = jnp.zeros(bgot.shape, f32)

    barrier = pltpu.get_barrier_semaphore()
    total = 0
    for k, a in enumerate(axes):
        for d in range(1, counts[k]):
            pl.semaphore_signal(
                barrier, inc=1, device_id={a: lax.rem(me[k] + d, counts[k])}, device_id_type=MESH
            )
            total += 1

    def split_store(ref, index, value):
        high = value.astype(bf16)
        ref[index + (0,)] = high
        ref[index + (1,)] = (value - high.astype(f32)).astype(bf16)

    KC = SPF * SY
    def ext_q(q):
        return jnp.where(q < PY, q, jnp.where(q < PY + 2, q - PY - 2, q - 2))

    rows, cols = iota((5 * QE, KC), 0), iota((5 * QE, KC), 1)
    split_store(wf_v, (), weight(cols // SY, rows // QE - 2, SPF)
                * weight(cols % SY, ext_q(rows % QE), SPF))
    rows, cols = iota((4 * QC, KC), 0), iota((4 * QC, KC), 1)
    along_y = weight(cols % SY + me[1] * SY, rows % QC, SPC)
    for ph in range(SPC // SPF):
        first = -2 if ph < SPC // SPF // 2 else -1
        split_store(wc_v, (ph,),
                    weight(cols // SY + ph * SPF, rows // QC + first, SPC) * along_y)

    pl.semaphore_wait(barrier, total)

    has = [(me[k] > 0, me[k] < counts[k] - 1) for k in range(3)]
    pieces = ys_sem.shape[1]
    each = SX // pieces

    def halo(k, side, piece=0):
        if k == 1:
            part = pl.ds(piece * each, each)
            return neighbour_copy(
                k, side, ysend.at[side, part], yrecv.at[1 - side, part],
                ys_sem.at[side, piece], yr_sem.at[1 - side, piece])
        if k == 0:
            src = s_v.at[pl.ds(2 if side == 0 else SX, 2), pl.ds(8, SY), :]
            dst = s_v.at[pl.ds(SX + 2 if side == 0 else 0, 2), pl.ds(8, SY), :]
        else:
            src, dst = zsend.at[side], zrecv.at[1 - side]
        return neighbour_copy(k, side, src, dst, hs_sem.at[k, side], hr_sem.at[k, 1 - side])

    def neighbour_copy(k, side, src, dst, send, recv):
        other = me[k] - 1 if side == 0 else me[k] + 1
        return pltpu.make_async_remote_copy(
            src_ref=src, dst_ref=dst, send_sem=send, recv_sem=recv,
            device_id={axes[k]: other}, device_id_type=MESH,
        )

    def start_halo(k, side, piece=0):
        @pl.when(has[k][side])
        def _():
            halo(k, side, piece).start()

    lane = iota((SY, SZ), 1)

    def one_slab(x, carry):
        low, high = carry
        s = w_v[x] + f_v[x]
        s_v[x + 2, 8:8 + SY, :] = s
        ysend[0, x] = s[0:2]
        ysend[1, x] = s[SY - 2:SY]
        here = lane // 2 == x
        low = jnp.where(here, pltpu.roll(s, 2 * x, 1), low)
        high = jnp.where(here, pltpu.roll(s, lax.rem(2 * x + 2, SZ), 1), high)
        return low, high

    carry = (jnp.zeros((SY, SZ), f32), jnp.zeros((SY, SZ), f32))
    done = set()
    sent = set()
    for c in order:
        for copy in loads[c]:
            copy.wait()
        carry = lax.fori_loop(c * SPF, (c + 1) * SPF, one_slab, carry)
        done.add(c)
        for piece in range(pieces):
            inside = range(piece * each // SPF, (piece + 1) * each // SPF)
            if piece not in sent and all(n in done for n in inside):
                sent.add(piece)
                start_halo(1, 0, piece)
                start_halo(1, 1, piece)
        if c == 0:
            start_halo(0, 0)
        if c == cells - 1:
            start_halo(0, 1)
    zsend[0] = carry[0]
    zsend[1] = carry[1]
    start_halo(2, 0)
    start_halo(2, 1)

    accf[...] = jnp.zeros(accf.shape, f32)
    accc[...] = jnp.zeros(accc.shape, f32)
    for copy in small:
        copy.wait()
    shape = (EX * QE, PX * PY)
    rows, cols = iota(shape, 0), iota(shape, 1)
    ox, oy = me[0] * PX, me[1] * PY
    outer, inner = rows // (EX * PY), rows % (EX * PY)
    planes = bend_planes(inner // PY - 2 + ox, ext_q(inner % PY + PY * outer) + oy,
                         cols // PY + ox, cols % PY + oy, PX * nx, PY * ny)
    RZ = tz_v.shape[2]

    def ext_point(row):
        return jnp.where(row < PZ, row, jnp.where(row < PZ + 2, row - PZ - 2, row - 2))

    oz = me[2] * PZ
    zr, zc = ext_point(iota((RZ, PZ), 0)) + oz, iota((RZ, PZ), 1) + oz
    along = (same(zr, zc), diff1(zr, zc), diff2(zr, zc, PZ * nz))
    for a in range(3):
        block = fc_ref[a].reshape(PX * PY, PZ)
        factors = [nn(plane, block) for plane in planes]
        for half in range(2):
            part = slice(half * EX * PY, (half + 1) * EX * PY)
            bend_v[half, a] = (nt(along[0], factors[0][part]) + nt(along[1], factors[1][part])
                               + nt(along[2], factors[2][part]))
    shape = (KX * QC, KX * QC)
    rows, cols = iota(shape, 0), iota(shape, 1)
    planes = bend_planes(rows // QC, rows % QC, cols // QC, cols % QC, KX, KY)
    zr, zc = iota((KZ, KZ), 0), iota((KZ, KZ), 1)
    for a in range(3):
        for p in range(KX):
            ccp[a, p * QC:p * QC + KY, :] = cc_ref[a, p]
        block = ccp[a]
        bendc[a] = (nn(planes[0], block) + nn(planes[1], nn(block, diff1(zr, zc)))
                    + BEND * nn(block, diff2(zr, zc, KZ)))

    for k in (0, 1, 2):
        for side in range(2):
            for piece in range(pieces if k == 1 else 1):
                @pl.when(has[k][side])
                def _(k=k, side=side, piece=piece):
                    halo(k, side, piece).wait_send()

                @pl.when(has[k][1 - side])
                def _(k=k, side=side, piece=piece):
                    halo(k, side, piece).wait_recv()

    even = lane % 2 == 0
    dl = zrecv[0] - zsend[1]
    dh = zrecv[1] - zsend[0]
    zcorr[0] = jnp.where(even, dl - 8.0 * pltpu.roll(dl, SZ - 1, 1), dl)
    zcorr[1] = jnp.where(even, -dh, 8.0 * pltpu.roll(dh, 1, 1) - dh)

    def forces(i):
        slot = i % 2
        for xx in range(SPF):
            x = i * SPF + xx
            s_v[x + 2, 6:8, :] = yrecv[0, x]
            s_v[x + 2, 8 + SY:10 + SY, :] = yrecv[1, x]
            d = w_v[x] - f_v[x]
            s = s_v[x + 2, 8:8 + SY, :]
            gx = (s_v[x, 8:8 + SY, :] - s_v[x + 4, 8:8 + SY, :]
                  + 8.0 * (s_v[x + 3, 8:8 + SY, :] - s_v[x + 1, 8:8 + SY, :]))
            gy = (s_v[x + 2, 6:6 + SY, :] - s_v[x + 2, 10:10 + SY, :]
                  + 8.0 * (s_v[x + 2, 9:9 + SY, :] - s_v[x + 2, 7:7 + SY, :]))
            gz = (pltpu.roll(s, 2, 1) - pltpu.roll(s, SZ - 2, 1)
                  + 8.0 * (pltpu.roll(s, SZ - 1, 1) - pltpu.roll(s, 1, 1)))
            corr = jnp.where(lane < 2, pltpu.roll(zcorr[0], (SZ - 2 * x) % SZ, 1), 0.0)
            corr = jnp.where(lane >= SZ - 2,
                             pltpu.roll(zcorr[1], (2 * SZ - 2 - 2 * x) % SZ, 1), corr)
            gz = gz + corr
            for a, g in enumerate((gx, gy, gz)):
                force = g * d
                high = force.astype(bf16)
                fh_v[slot, xx * SY:(xx + 1) * SY, a * SZ:(a + 1) * SZ] = high
                fl_v[slot, xx * SY:(xx + 1) * SY, a * SZ:(a + 1) * SZ] = (
                    force - high.astype(f32)).astype(bf16)

    def gather(i):
        slot = i % 2
        k, ph = divmod(i, SPC // SPF)
        many = 5 * QE + 4 * QC
        weights = jnp.concatenate([wf_v[0], wc_v[ph, 0], wf_v[1], wc_v[ph, 1]], axis=0)
        both = jnp.dot(weights, fh_v[slot], preferred_element_type=f32)
        out = both[:many] + both[many:] + jnp.dot(
            weights[:many], fl_v[slot], preferred_element_type=f32)
        fine = out[:5 * QE].reshape(5, 2, PY, lanes)
        accf[0, i:i + 5] += fine[:, 0]
        accf[1, i:i + 5] += fine[:, 1]
        at = me[0] * (SX // SPC) + k + (1 if ph >= SPC // SPF // 2 else 0)
        accc[pl.ds(at, 4)] += out[5 * QE:].reshape(4, QC, lanes)

    forces(0)
    for i in range(cells):
        if i + 1 < cells:
            forces(i + 1)
        gather(i)

    rows, cols = iota((RZ, SZ), 0), iota((RZ, SZ), 1)
    bz = weight(cols, ext_point(rows), SPF) * (SPF ** -1.5 / 24.0)
    rows, cols = iota((KZ, SZ), 0), iota((KZ, SZ), 1)
    bzc = weight(cols + me[2] * SZ, rows, SPC) * (SPC ** -1.5 / 24.0)
    for a in range(3):
        for half in range(2):
            block = accf[half, :, :, a * SZ:(a + 1) * SZ].reshape(EX * PY, SZ)
            tz_v[half, a] = nt(bz, block) + bend_v[half, a]
            for side in range(2):
                zmsg[side, half, 2 * a:2 * a + 2, :] = tz_v[
                    half, a, PZ + 2 * side:PZ + 2 * side + 2, :]
    blocks = [accc[2:2 + KX, :, a * SZ:(a + 1) * SZ].reshape(KX * QC, SZ) for a in range(3)]
    cslots[2, me[2]] = nt(bzc, jnp.concatenate(blocks, axis=0))

    def coarse_copy(k, d, slot):
        n = counts[k]
        return pltpu.make_async_remote_copy(
            src_ref=cslots.at[k, slot], dst_ref=cslots.at[k, slot],
            send_sem=cs_sem.at[k, d], recv_sem=cr_sem.at[k, d],
            device_id={axes[k]: lax.rem(me[k] + d, n)}, device_id_type=MESH,
        )

    def exchange(k, source, got):
        for side in range(2):
            @pl.when(has[k][side])
            def _(side=side):
                neighbour_copy(k, side, source(side), got.at[1 - side],
                               ms_sem.at[k, side], mr_sem.at[k, 1 - side]).start()
        for d in range(1, counts[k]):
            coarse_copy(k, d, me[k]).start()
        for side in range(2):
            @pl.when(has[k][side])
            def _(side=side):
                neighbour_copy(k, side, source(side), got.at[1 - side],
                               ms_sem.at[k, side], mr_sem.at[k, 1 - side]).wait_send()

            @pl.when(has[k][1 - side])
            def _(side=side):
                neighbour_copy(k, side, source(side), got.at[1 - side],
                               ms_sem.at[k, side], mr_sem.at[k, 1 - side]).wait_recv()
        for d in range(1, counts[k]):
            coarse_copy(k, d, me[k]).wait_send()
            coarse_copy(k, d, lax.rem(me[k] + counts[k] - d, counts[k])).wait_recv()
        whole = cslots[k, 0]
        for n in range(1, counts[k]):
            whole = whole + cslots[k, n]
        return whole

    whole = exchange(2, lambda side: zmsg.at[side], zgot)
    for half in range(2):
        for a in range(3):
            tz_v[half, a, 0:2, :] = tz_v[half, a, 0:2, :] + zgot[0, half, 2 * a:2 * a + 2, :]
            tz_v[half, a, PZ - 2:PZ, :] = (
                tz_v[half, a, PZ - 2:PZ, :] + zgot[1, half, 2 * a:2 * a + 2, :])
            a_v[half, a * PZ:(a + 1) * PZ, :] = tz_v[half, a, 0:PZ, :]

    cslots[1, me[1]] = whole
    whole = exchange(1, lambda side: a_v.at[1], agot)
    shape = (EX * PY, EX * PY)
    rows, cols = iota(shape, 0), iota(shape, 1)
    p_same = rows // PY == cols // PY
    q, r = rows % PY, cols % PY
    low = jnp.where(p_same & (q == r + 2) & (r < 2), 1.0, 0.0)
    high = jnp.where(p_same & (q == r - (PY - 2)) & (r >= PY - 2), 1.0, 0.0)
    b_v[...] = a_v[0] + nn(agot[0], low) + nn(agot[1], high)

    cslots[0, me[0]] = whole
    whole = exchange(0, lambda side: b_v, bgot)
    shape = (PX * PY, EX * PY)
    rows, cols = iota(shape, 0), iota(shape, 1)
    own = jnp.where(cols == rows + 2 * PY, 1.0, 0.0)
    low = jnp.where((cols == rows + (PX + 2) * PY) & (rows < 2 * PY), 1.0, 0.0)
    high = jnp.where((cols == rows - (PX - 2) * PY) & (rows >= (PX - 2) * PY), 1.0, 0.0)
    shape = (3 * KX * QC, 3 * KX * QC)
    turned = nt(same(iota(shape, 0), iota(shape, 1)), whole)
    for a in range(3):
        part = slice(a * PZ, (a + 1) * PZ)
        out = nt(own, b_v[part]) + nt(low, bgot[0, part]) + nt(high, bgot[1, part])
        fo_ref[a] = out.reshape(PX, PY, PZ)
        out = turned[a * KX * QC:(a + 1) * KX * QC] + bendc[a]
        for p in range(KX):
            co_ref[a, p] = out[p * QC:p * QC + KY, :]


def solution(mesh):
    sizes = tuple(mesh.shape[a] for a in ("gx", "gy", "gz"))

    def step(warped, fixed, fine, coarse):
        SX, SY, SZ = warped.shape
        PX, PY, PZ = SX // SPF, SY // SPF, SZ // SPF
        KX, KY, KZ = coarse.shape[1:]
        QC = KY
        EX, QE, RZ = PX + 4, 2 * PY, PZ + 8
        KC = SPF * SY
        most = max(sizes)
        vmem = pl.BlockSpec(memory_space=pltpu.VMEM)
        hbm = pl.BlockSpec(memory_space=pltpu.HBM)
        V = pltpu.VMEM
        D = pltpu.SemaphoreType.DMA
        return pl.pallas_call(
            functools.partial(kernel, sizes),
            out_shape=(jax.ShapeDtypeStruct(fine.shape, f32),
                       jax.ShapeDtypeStruct(coarse.shape, f32)),
            in_specs=[hbm] * 4,
            out_specs=(vmem, vmem),
            scratch_shapes=[
                V((SX, SY, SZ), f32), V((SX, SY, SZ), f32),
                V((3, PX, PY, PZ), f32), V(coarse.shape, f32),
                V((SX + 4, SY + 16, SZ), f32),
                V((2, SX, 2, SZ), f32), V((2, SX, 2, SZ), f32),
                V((2, SY, SZ), f32), V((2, SY, SZ), f32), V((2, SY, SZ), f32),
                V((2, 5 * QE, KC), bf16), V((SPC // SPF, 2, 4 * QC, KC), bf16),
                V((2, KC, 3 * SZ), bf16), V((2, KC, 3 * SZ), bf16),
                V((2, EX, PY, 3 * SZ), f32), V((KX + 4, QC, 3 * SZ), f32),
                V((2, 3, RZ, EX * PY), f32), V((2, 3, RZ, EX * PY), f32),
                V((3, KX * QC, KZ), f32), V((3, KX * QC, KZ), f32),
                V((2, 2, 8, EX * PY), f32), V((2, 2, 8, EX * PY), f32),
                V((2, 3 * PZ, EX * PY), f32), V((2, 3 * PZ, EX * PY), f32),
                V((3 * PZ, EX * PY), f32), V((2, 3 * PZ, EX * PY), f32),
                V((3, most, KZ, 3 * KX * QC), f32),
                D((2, SX // SPF)), D((2,)), D((3, 2)), D((3, 2)), D((2, 4)), D((2, 4)),
                D((3, 2)), D((3, 2)), D((3, most)), D((3, most)),
            ],
            compiler_params=pltpu.CompilerParams(
                collective_id=0, has_side_effects=True, vmem_limit_bytes=66000000
            ),
        )(warped, fixed, fine, coarse)

    in_specs = (P("gx", "gy", "gz"), P("gx", "gy", "gz"), P(None, "gx", "gy", "gz"), P())
    out_specs = (P(None, "gx", "gy", "gz"), P())
    return jax.shard_map(
        step, mesh=mesh, in_specs=in_specs, out_specs=out_specs, check_vma=False
    )
```

profile of v0, /device:TPU:0, one launch (start us, length us, event | category | flops | bytes accessed | tf_op | source)
XLA Modules:
  0.0 35.1 jit_solution(13479825486412277418)
XLA Ops:
  0.6 31.5 %shard_map.59 = (f32[3,8,8,16]{3,2,1,0:T(8,128)}, f32[3,8,4,16]{3,2,1,0:T(4,128)}) custom-call(f32[64,64,128]{2,1,0:T(8,128)} %w_hbm.1, f32[64,64,128]{2,1,0:T(8,128)} %f_hbm.1, f32[3,8,8,16]{3,2,1,0:T(8,128)} %fc_hbm.1, f32[3,8,4,16]{3,2,1,0:T(4,128)} %cc_hbm.1), custom_call_target="tpu_custom_call" | custom-call | tf_op jit(solution)/shard_map/pallas_call | solution.py:408
  32.1 1.5 %copy.8 = f32[3,8,8,16]{3,2,1,0:T(8,128)} copy(f32[3,8,8,16]{3,2,1,0:T(8,128)} %get-tuple-element.4) | data formatting | bytes 24576
  33.7 1.4 %copy.9 = f32[3,8,4,16]{3,2,1,0:T(4,128)} copy(f32[3,8,4,16]{3,2,1,0:T(4,128)} %get-tuple-element.5) | data formatting | bytes 12288
where the time goes:
time: 35.3 us; the launch traced here: 35.1 us
  Pallas kernels  31.5 us (89%)
  local copies, waits for them, and re-layouts  2.96 us (8%)
  between operations  0.64 us (2%)
    pallas_call x1, Pallas kernels, step(): pl.pallas_call(functools.partial(kernel, sizes), out_shape=(jax.ShapeDtyp...  31.5 us
    unnamed x2, local copies, waits for them, and re-layouts  2.96 us

commit v1 on v0

--- a/solution.py
+++ b/solution.py
@@ -390,6 +390,11 @@
             co_ref[a, p] = out[p * QC:p * QC + KY, :]
 
 
+def write_out(f_ref, c_ref, fo_ref, co_ref):
+    fo_ref[...] = f_ref[...]
+    co_ref[...] = c_ref[...]
+
+
 def solution(mesh):
     sizes = tuple(mesh.shape[a] for a in ("gx", "gy", "gz"))
 
@@ -405,10 +410,9 @@
         hbm = pl.BlockSpec(memory_space=pltpu.HBM)
         V = pltpu.VMEM
         D = pltpu.SemaphoreType.DMA
-        return pl.pallas_call(
+        held = pl.pallas_call(
             functools.partial(kernel, sizes),
-            out_shape=(jax.ShapeDtypeStruct(fine.shape, f32),
-                       jax.ShapeDtypeStruct(coarse.shape, f32)),
+            out_shape=(pltpu.VMEM(fine.shape, f32), pltpu.VMEM(coarse.shape, f32)),
             in_specs=[hbm] * 4,
             out_specs=(vmem, vmem),
             scratch_shapes=[
@@ -433,6 +437,14 @@
                 collective_id=0, has_side_effects=True, vmem_limit_bytes=66000000
             ),
         )(warped, fixed, fine, coarse)
+        held = [pltpu.with_memory_space_constraint(h, memory_space=pltpu.VMEM) for h in held]
+        return pl.pallas_call(
+            write_out,
+            out_shape=(jax.ShapeDtypeStruct(fine.shape, f32),
+                       jax.ShapeDtypeStruct(coarse.shape, f32)),
+            in_specs=[vmem] * 2,
+            out_specs=(vmem, vmem),
+        )(*held)
 
     in_specs = (P("gx", "gy", "gz"), P("gx", "gy", "gz"), P(None, "gx", "gy", "gz"), P())
     out_specs = (P(None, "gx", "gy", "gz"), P())

time: 35.3 us -> 32.3 us (0.915)
  local copies, waits for them, and re-layouts: 2.96 us -> 0 us
    unnamed x2 -> x0, local copies, waits for them, and re-layouts: 2.96 us -> none
    pallas_call x1 -> x2, Pallas kernels: 31.5 us -> 31.5 us  [the longest x1 30.9 us: step(): pl.pallas_call(functools.partial(kernel, sizes), out_shape=(pltpu.VMEM(fi...]
where the time goes in v1:
time: 32.3 us; the launch traced here: 32.2 us
  Pallas kernels  31.5 us (98%)
  between operations  0.64 us (2%)
    pallas_call x1, Pallas kernels, step(): pl.pallas_call(functools.partial(kernel, sizes), out_shape=(pltpu.VMEM(fi...  30.9 us
    pallas_call x1, Pallas kernels, step(): pl.pallas_call(write_out, out_shape=(jax.ShapeDtypeStruct(fine.shape, f32...  0.67 us

profile of v1, /device:TPU:0, one launch (start us, length us, event | category | flops | bytes accessed | tf_op | source)
XLA Modules:
  0.0 32.2 jit_solution(3825871965653791436)
XLA Ops:
  0.6 30.9 %shard_map.59 = (f32[3,8,8,16]{3,2,1,0:T(8,128)S(1)}, f32[3,8,4,16]{3,2,1,0:T(4,128)S(1)}) custom-call(f32[64,64,128]{2,1,0:T(8,128)} %w_hbm.1, f32[64,64,128]{2,1,0:T(8,128)} %f_hbm.1, f32[3,8,8,16]{3,2,1,0:T(8,128)} %fc_hbm.1, f32[3,8,4,16]{3,2,1,0:T(4,128)} %cc_hbm.1), custom_call_target="tpu_custom_call" | custom-call | tf_op jit(solution)/shard_map/pallas_call | solution.py:413
  31.5 0.7 %shard_map.60 = (f32[3,8,8,16]{3,2,1,0:T(8,128)}, f32[3,8,4,16]{3,2,1,0:T(4,128)}) custom-call(f32[3,8,8,16]{3,2,1,0:T(8,128)S(1)} %get-tuple-element.4.f_ref, f32[3,8,4,16]{3,2,1,0:T(4,128)S(1)} %get-tuple-element.5.c_ref), custom_call_target="tpu_custom_call" | custom-call | tf_op jit(solution)/shard_map/pallas_call | solution.py:441

commit v2 on v1

v2 whole, which is shorter than its diff:
```python
import functools

import jax
import jax.numpy as jnp
from jax import lax
from jax.experimental import pallas as pl
from jax.experimental.pallas import tpu as pltpu
from jax.sharding import PartitionSpec as P

SPF = 8
SPC = 32
BEND = 0.01
MESH = pl.DeviceIdType.MESH
f32 = jnp.float32
bf16 = jnp.bfloat16
AXES = ("gx", "gy", "gz")
SIDES = (0, 1)
AROUND = [(dx, dy) for dx in (-1, 0, 1) for dy in (-1, 0, 1) if dx or dy]


def dot(a, b):
    return jnp.dot(a, b, preferred_element_type=f32)


def spline(t):
    m = jnp.abs(t)
    inner = 2.0 / 3.0 - m * m + 0.5 * m * m * m
    r = jnp.maximum(2.0 - m, 0.0)
    outer = r * r * r * (1.0 / 6.0)
    return jnp.where(m < 1.0, inner, outer)


def weight(voxel, point, spacing):
    scaled = (2 * voxel + 1 - spacing * (2 * point + 1)).astype(f32)
    return spline(scaled * (0.5 / spacing))


def iota(shape, axis):
    return lax.broadcasted_iota(jnp.int32, shape, axis)


def split2(value):
    high = value.astype(bf16)
    return high, (value - high.astype(f32)).astype(bf16)


def split3(value):
    high = value.astype(bf16)
    rest = value - high.astype(f32)
    mid = rest.astype(bf16)
    return high, mid, (rest - mid.astype(f32)).astype(bf16)


def same(out, inp):
    return jnp.where(out == inp, 1.0, 0.0).astype(f32)


def diff1(out, inp):
    d = jnp.abs(out - inp)
    return jnp.where(d == 0, -2.0, jnp.where(d == 1, 1.0, 0.0)).astype(f32)


def diff2(out, inp, count):
    d = jnp.abs(out - inp)
    edge = (inp == 0) | (inp == count - 1)
    centre = jnp.where(edge, 5.0, 6.0)
    return jnp.where(
        d == 0, centre, jnp.where(d == 1, -4.0, jnp.where(d == 2, 1.0, 0.0))
    ).astype(f32)


def cross(ref, x, rows):
    first, count = rows
    here = ref[x, first:first + count]
    return (ref[x - 1, first:first + count] + ref[x + 1, first:first + count]
            + ref[x, first - 1:first - 1 + count] + ref[x, first + 1:first + 1 + count]
            - 4.0 * here), here


def kernel(sizes, w_hbm, f_hbm, fc_hbm, cc_hbm, fo_ref, co_ref,
           w_v, f_v, fc_ref, cc_ref, s_v, ysend, yrecv, zsend, zrecv, dz_v,
           wf_v, wc_v, wy_v, wq_v, wx_v, wz_v, wh_v, fh_v, fl_v,
           accf, accc, pad_v, mid_v, bend_v, padc_v, midc_v, bendc_v,
           part_v, zm_v, zg_v, zt_v, g_v, xm_v, ym_v, xg_v, yg_v, cg_v,
           cz_v, cp_v,
           load_sem, small_sem, hs_sem, hr_sem, ys_sem, yr_sem,
           ms_sem, mr_sem, as_sem, ar_sem, cs_sem, cr_sem, ps_sem, pr_sem):
    nx, ny, nz = sizes
    me = [lax.axis_index(a) for a in AXES]
    SX, SY, SZ = w_v.shape
    PX, PY, PZ = SX // SPF, SY // SPF, SZ // SPF
    KX, KY, KZ = cc_ref.shape[1:]
    EX, QE = PX + 4, PY + 8
    XC, QC = accc.shape[:2]
    cells = SX // SPF
    per = SPC // SPF
    lanes = 3 * SZ
    NF, NC = EX * QE, XC * QC
    LW = 128
    has = [(me[k] > 0, me[k] < sizes[k] - 1) for k in range(3)]

    small = (pltpu.make_async_copy(fc_hbm, fc_ref, small_sem.at[0]),
             pltpu.make_async_copy(cc_hbm, cc_ref, small_sem.at[1]))
    for copy in small:
        copy.start()
    loads = []
    for c in range(cells):
        part = pl.ds(c * SPF, SPF)
        loads.append((
            pltpu.make_async_copy(w_hbm.at[part], w_v.at[part], load_sem.at[0, c]),
            pltpu.make_async_copy(f_hbm.at[part], f_v.at[part], load_sem.at[1, c]),
        ))
    order = [0, cells - 1] + list(range(1, cells - 1))
    for c in order:
        loads[c][0].start()
        loads[c][1].start()

    barrier = pltpu.get_barrier_semaphore()
    total = 0
    plane = [(ox, oy) for ox in range(nx) for oy in range(ny) if ox or oy]

    def in_plane(ox, oy):
        return {"gx": lax.rem(me[0] + ox, nx), "gy": lax.rem(me[1] + oy, ny)}

    for d in range(1, nz):
        pl.semaphore_signal(
            barrier, inc=1, device_id={"gz": lax.rem(me[2] + d, nz)}, device_id_type=MESH)
        total += 1
    for ox, oy in plane:
        pl.semaphore_signal(barrier, inc=1, device_id=in_plane(ox, oy), device_id_type=MESH)
        total += 1

    s_v[2:SX + 2, 0:8, :] = jnp.zeros((SX, 8, SZ), f32)
    s_v[2:SX + 2, 8 + SY:16 + SY, :] = jnp.zeros((SX, 8, SZ), f32)
    accf[...] = jnp.zeros(accf.shape, f32)
    accc[...] = jnp.zeros(accc.shape, f32)
    pad_v[...] = jnp.zeros(pad_v.shape, f32)
    mid_v[...] = jnp.zeros(mid_v.shape, f32)
    padc_v[...] = jnp.zeros(padc_v.shape, f32)
    midc_v[...] = jnp.zeros(midc_v.shape, f32)
    zt_v[...] = jnp.zeros(zt_v.shape, f32)
    dz_v[...] = jnp.zeros(dz_v.shape, f32)
    zsend[...] = jnp.zeros(zsend.shape, f32)
    xpad = (pl.ds(0, 2), pl.ds(SX + 2, 2))

    def zero(ref, index):
        ref[index] = jnp.zeros(ref.at[index].shape, f32)

    for side in SIDES:
        @pl.when(jnp.logical_not(has[0][side]))
        def _(side=side):
            zero(s_v, (xpad[side], slice(8, 8 + SY)))
            zero(xg_v, side)
            for other in SIDES:
                zero(cg_v, (side, other))

        @pl.when(jnp.logical_not(has[1][side]))
        def _(side=side):
            zero(yrecv, side)
            zero(yg_v, side)
            for other in SIDES:
                zero(cg_v, (other, side))

        @pl.when(jnp.logical_not(has[2][side]))
        def _(side=side):
            zero(zrecv, side)
            zero(zg_v, side)

    def edge_row(row):
        return jnp.where(row < PY, row, jnp.where(row < PY + 2, row - PY - 2,
                         jnp.where(row < PY + 4, row - 2, row + 8 * PY)))

    def put(ref, index, value):
        high, low = split2(value)
        ref[(0,) + index] = high
        ref[(1,) + index] = low

    KV = SPF * SY
    cols = iota((QE, KV), 1)
    along_y = weight(cols % SY, edge_row(iota((QE, KV), 0)), SPF)
    along_x = weight(iota((8, KV), 1) // SY, iota((8, KV), 0) - 2, SPF)
    for p in range(5):
        put(wf_v, (slice(p * QE, (p + 1) * QE),), along_y * along_x[p:p + 1])
    rows, cols = iota((4 * QC, KV), 0), iota((4 * QC, KV), 1)
    along_y = weight(cols % SY + me[1] * SY, rows % QC, SPC)
    for ph in range(per):
        first = -2 if ph < per // 2 else -1
        along_x = weight(cols // SY + ph * SPF, rows // QC + first, SPC)
        high, low = split2(along_x * along_y)
        wc_v[ph, 0] = high
        wc_v[ph, 1] = low

    KH = 4 * SX
    place = (iota((16, KH), 1) // SX)
    yat = jnp.where(place < 2, place, SY - 4 + place)
    along_y = weight(yat, edge_row(iota((16, KH), 0)), SPF)
    along_x = weight(iota((16, KH), 1) % SX, iota((16, KH), 0) - 2, SPF)
    for p in range(EX):
        put(wy_v, (slice(p * QE, (p + 1) * QE),), along_y * along_x[p:p + 1])
    rows, cols = iota((NC, KH), 0), iota((NC, KH), 1)
    place = cols // SX
    yat = jnp.where(place < 2, place, SY - 4 + place)
    put(wy_v, (slice(NF, NF + NC),), weight(cols % SX, rows // QC - 2, SPC)
        * weight(yat + me[1] * SY, rows % QC, SPC))

    KP = 2 * SZ
    rows, cols = iota((QE, SY), 0), iota((QE, SY), 1)
    put(wq_v, (slice(0, QE),), weight(cols, edge_row(rows), SPF))
    rows, cols = iota((QC, SY), 0), iota((QC, SY), 1)
    put(wq_v, (slice(QE, QE + QC),), weight(cols + me[1] * SY, rows, SPC))
    col = iota((EX, KP), 1)
    xat = jnp.where(col < SZ, (col + SZ - 2) % SZ, col % SZ) // 2
    wx_v[0:EX] = weight(xat, iota((EX, KP), 0) - 2, SPF)
    wx_v[EX:EX + XC] = weight(xat[0:XC], iota((XC, KP), 0) - 2, SPC)

    def fine_lane(l):
        e = (l - 3 * PZ) % 8
        centre = l < 3 * PZ
        known = centre | ((l < 3 * PZ + 16) & (e < 6))
        comp = jnp.where(centre, l // PZ, jnp.where(known, e // 2, 3))
        point = jnp.where(centre, l % PZ, jnp.where(l < 3 * PZ + 8, e % 2 - 2, PZ + e % 2))
        return comp, point

    def both_levels(z):
        l = iota(z.shape, 1)[:, 0:LW]
        z = z[:, 0:LW]
        comp, point = fine_lane(l)
        fine = weight(z, point, SPF) * (SPF ** -1.5 / 24.0)
        ccomp = l // KZ
        coarse = weight(z + me[2] * SZ, l % KZ, SPC) * (SPC ** -1.5 / 24.0)
        return jnp.concatenate([comp, ccomp], 1), jnp.concatenate([fine, coarse], 1)

    comp, value = both_levels(iota((SZ, 2 * LW), 0))
    high, low = split2(value)
    high, low = high.astype(f32), low.astype(f32)
    for a in range(3):
        part = slice(a * SZ, (a + 1) * SZ)
        wz_v[0, part] = jnp.where(comp == a, high, 0.0).astype(bf16)
        wz_v[1, part] = jnp.where(comp == a, low, 0.0).astype(bf16)
    row = iota((8, 2 * LW), 0)
    comp, value = both_levels(jnp.where(row < 2, row, SZ - 4 + row))
    value = jnp.where(comp == 2, value, 0.0)
    odd = iota((SZ, 2 * LW), 0) % 2 == 1
    for side in SIDES:
        part = slice(side * SZ, (side + 1) * SZ)
        put(wh_v, (part,), jnp.where(odd, value[2 * side + 1:2 * side + 2],
                                     value[2 * side:2 * side + 1]))

    for copy in small:
        copy.wait()

    def spread(ref, a, count, width, matrix):
        block = ref[a].reshape(count, width)
        return sum(dot(part, matrix) for part in split3(block))

    zin, l = iota((PZ, LW), 0), iota((PZ, LW), 1)
    comp, point = fine_lane(l)
    oz = me[2] * PZ
    shares = 0.0
    for a in range(3):
        m = jnp.concatenate([same(point, zin), 2.0 * diff1(point, zin),
                             diff2(point + oz, zin + oz, PZ * nz)], 1)
        ok = jnp.concatenate([comp == a] * 3, 1)
        shares = shares + spread(fc_ref, a, PX * PY, PZ, jnp.where(ok, m, 0.0).astype(bf16))
    shares = shares.reshape(PX, PY, 3 * LW)
    pad_v[3:3 + PX, 8:8 + PY, :] = shares[:, :, 0:LW]
    inside = iota((PY + 8, LW), 0) - 4 + me[1] * PY
    inside = (inside >= 0) & (inside < PY * ny)
    for p in range(-1, PX + 1):
        u, _ = cross(pad_v, 3 + p, (4, PY + 8))
        keep = inside & (me[0] * PX + p >= 0) & (me[0] * PX + p < PX * nx)
        mid_v[3 + p, 4:12 + PY] = jnp.where(keep, u, 0.0)
    mid_v[3:3 + PX, 8:8 + PY, :] = mid_v[3:3 + PX, 8:8 + PY, :] + shares[:, :, LW:2 * LW]
    row = iota((PY, LW), 0)
    for p in range(-2, PX + 2):
        v = [cross(mid_v, 3 + p, (first, PY))[0] for first in (8, 6, 6 + PY)]
        centre = v[0]
        if 0 <= p < PX:
            centre = centre + shares[p, :, 2 * LW:3 * LW]
        bend_v[2 + p, 0:PY] = centre * BEND
        bend_v[2 + p, PY:2 * PY] = jnp.where(
            row < 2, v[1], jnp.where(row < 4, v[2], 0.0)) * BEND

    pieces = ys_sem.shape[1]
    each = SX // pieces

    def neighbour_copy(k, side, src, dst, send, recv):
        other = me[k] - 1 if side == 0 else me[k] + 1
        return pltpu.make_async_remote_copy(
            src_ref=src, dst_ref=dst, send_sem=send, recv_sem=recv,
            device_id={AXES[k]: other}, device_id_type=MESH,
        )

    def halo(k, side, piece=0):
        if k == 1:
            part = pl.ds(piece * each, each)
            return neighbour_copy(
                k, side, ysend.at[side, :, part], yrecv.at[1 - side, :, part],
                ys_sem.at[side, piece], yr_sem.at[1 - side, piece])
        if k == 0:
            src = s_v.at[pl.ds(2 if side == 0 else SX, 2), pl.ds(8, SY), :]
            dst = s_v.at[pl.ds(SX + 2 if side == 0 else 0, 2), pl.ds(8, SY), :]
        else:
            src, dst = zsend.at[side], zrecv.at[1 - side]
        return neighbour_copy(k, side, src, dst, hs_sem.at[k, side], hr_sem.at[k, 1 - side])

    def start_halo(k, side, piece=0):
        @pl.when(has[k][side])
        def _():
            halo(k, side, piece).start()

    def wait_halo(k):
        for side in SIDES:
            for piece in range(pieces if k == 1 else 1):
                @pl.when(has[k][side])
                def _(side=side, piece=piece):
                    halo(k, side, piece).wait_send()

                @pl.when(has[k][1 - side])
                def _(side=side, piece=piece):
                    halo(k, side, piece).wait_recv()

    tile_lane = iota((8, SZ), 1)
    srows = s_v.reshape((SX + 4) * (SY + 16), SZ)
    drows = w_v.reshape(SX * SY, SZ)

    def sums(c):
        for copy in loads[c]:
            copy.wait()
        for y in range(0, SY, 8):
            rows = slice(y, y + 8)
            packs = [zsend[0, rows], zsend[1, rows], dz_v[0, rows], dz_v[1, rows]]
            for x in range(c * SPF, (c + 1) * SPF):
                w, f = w_v[x, rows], f_v[x, rows]
                s, d = w + f, w - f
                s_v[x + 2, 8 + y:16 + y] = s
                w_v[x, rows] = d
                shift = (2 * x + 2) % SZ
                s, d = pltpu.roll(s, shift, 1), pltpu.roll(d, shift, 1)
                low = tile_lane // 2 == (x + 1) % (SZ // 2)
                high = tile_lane // 2 == x
                packs = [jnp.where(low, s, packs[0]), jnp.where(high, s, packs[1]),
                         jnp.where(low, d, packs[2]), jnp.where(high, d, packs[3])]
            zsend[0, rows], zsend[1, rows], dz_v[0, rows], dz_v[1, rows] = packs

    def yfaces(piece):
        for side in SIDES:
            for k in range(2):
                y = k if side == 0 else SY - 2 + k
                ysend[side, k, pl.ds(piece * each, each)] = srows[
                    pl.ds((piece * each + 2) * (SY + 16) + 8 + y, each, stride=SY + 16), :]
            start_halo(1, side, piece)

    def forces(i, slot):
        for xx in range(SPF):
            x = i * SPF + xx
            d = w_v[x]
            s = s_v[x + 2, 8:8 + SY, :]
            gx = (s_v[x, 8:8 + SY, :] - s_v[x + 4, 8:8 + SY, :]
                  + 8.0 * (s_v[x + 3, 8:8 + SY, :] - s_v[x + 1, 8:8 + SY, :]))
            gy = (s_v[x + 2, 6:6 + SY, :] - s_v[x + 2, 10:10 + SY, :]
                  + 8.0 * (s_v[x + 2, 9:9 + SY, :] - s_v[x + 2, 7:7 + SY, :]))
            gz = (pltpu.roll(s, 2, 1) - pltpu.roll(s, SZ - 2, 1)
                  + 8.0 * (pltpu.roll(s, SZ - 1, 1) - pltpu.roll(s, 1, 1)))
            for a, g in enumerate((gx, gy, gz)):
                high, low = split2(g * d)
                fh_v[slot, xx * SY:(xx + 1) * SY, a * SZ:(a + 1) * SZ] = high
                fl_v[slot, xx * SY:(xx + 1) * SY, a * SZ:(a + 1) * SZ] = low

    lane = iota((SY, SZ), 1)

    def gather(i, slot):
        k, ph = divmod(i, per)
        many = 5 * QE + 4 * QC
        weights = jnp.concatenate([wf_v[0], wc_v[ph, 0], wf_v[1], wc_v[ph, 1]], axis=0)
        both = dot(weights, fh_v[slot])
        out = both[:many] + both[many:] + dot(weights[:many], fl_v[slot])
        accf[i:i + 5] += out[:5 * QE].reshape(5, QE, lanes)
        at = k + (1 if ph >= per // 2 else 0)
        accc[at:at + 4] += out[5 * QE:].reshape(4, QC, lanes)

    summed, sent = set(), set()

    def run_sums(c):
        sums(c)
        summed.add(c)

    def run_faces():
        for piece in range(pieces):
            inside = range(piece * each // SPF, (piece + 1) * each // SPF)
            if piece not in sent and all(n in summed for n in inside):
                sent.add(piece)
                yfaces(piece)

    for c in order[:3]:
        run_sums(c)
    pl.semaphore_wait(barrier, total)
    start_halo(0, 0)
    start_halo(0, 1)
    run_faces()
    for c in order[3:]:
        run_sums(c)
        run_faces()
    start_halo(2, 0)
    start_halo(2, 1)

    turn = list(range(1, cells - 1)) + [0, cells - 1]
    forces(turn[0], 0)
    for n, i in enumerate(turn):
        if n + 1 < cells:
            if turn[n + 1] == 0:
                wait_halo(0)
            forces(turn[n + 1], (n + 1) % 2)
        gather(i, n % 2)

    wait_halo(1)
    wait_halo(2)
    adds = []
    for side in SIDES:
        h0, h1 = yrecv[side, 0], yrecv[side, 1]
        g = (h0 - 8.0 * h1, h1) if side == 0 else (-h0, 8.0 * h0 - h1)
        for k in range(2):
            y = k if side == 0 else SY - 2 + k
            adds.append(g[k] * drows[pl.ds(y, SX, stride=SY), :])
    high, low = split2(jnp.concatenate(adds, 0))
    weights = wy_v[0]
    added = dot(weights, high) + dot(wy_v[1], high) + dot(weights, low)

    even = lane % 2 == 0
    hl, hh = zrecv[0] - zsend[1], zrecv[1] - zsend[0]
    cl = jnp.where(even, hl - 8.0 * pltpu.roll(hl, SZ - 1, 1), hl)
    ch = jnp.where(even, -hh, 8.0 * pltpu.roll(hh, 1, 1) - hh)
    fz = jnp.concatenate([pltpu.roll(cl, 2, 1) * dz_v[0],
                          pltpu.roll(ch, SZ - 2, 1) * dz_v[1]], 1)
    high, low = split2(fz)
    g = dot(wq_v[0], high) + dot(wq_v[1], high) + dot(wq_v[0], low)
    blocks = [g[0:QE] * wx_v[p:p + 1] for p in range(EX)]
    blocks += [g[QE:QE + QC] * wx_v[EX + p:EX + p + 1] for p in range(XC)]
    hhigh, hlow = split2(jnp.concatenate(blocks, 0))

    table = jnp.concatenate([accf[...].reshape(NF, lanes), accc[...].reshape(NC, lanes)], 0)
    table = jnp.concatenate(
        [table[:, 0:SZ], table[:, SZ:2 * SZ] + added, table[:, 2 * SZ:]], 1)
    high, low = split2(table)
    whole = (dot(high, wz_v[0]) + dot(high, wz_v[1]) + dot(low, wz_v[0])
             + dot(hhigh, wh_v[0]) + dot(hhigh, wh_v[1]) + dot(hlow, wh_v[0]))

    cz_v[me[2]] = whole[NF:NF + NC, LW:2 * LW].reshape(XC, QC, LW)

    def coarse_z(d, slot):
        return pltpu.make_async_remote_copy(
            src_ref=cz_v.at[slot], dst_ref=cz_v.at[slot],
            send_sem=cs_sem.at[d], recv_sem=cr_sem.at[d],
            device_id={"gz": lax.rem(me[2] + d, nz)}, device_id_type=MESH)

    for d in range(1, nz):
        coarse_z(d, me[2]).start()

    fine = whole[0:NF, 0:LW] + bend_v[...].reshape(NF, LW)
    part_v[...] = fine
    tall = jnp.concatenate([fine, jnp.zeros((2 * LW - NF, LW), f32)], 0).T
    for side in SIDES:
        zm_v[side] = tall[3 * PZ + 8 * side:3 * PZ + 8 * side + 8]

    def fine_z(side):
        return neighbour_copy(2, side, zm_v.at[side], zg_v.at[1 - side],
                              ms_sem.at[side], mr_sem.at[1 - side])

    for side in SIDES:
        @pl.when(has[2][side])
        def _(side=side):
            fine_z(side).start()

    zin, l = iota((KZ, LW), 0), iota((KZ, LW), 1)
    shares = 0.0
    for a in range(3):
        m = jnp.concatenate([same(l % KZ, zin), 2.0 * diff1(l % KZ, zin),
                             diff2(l % KZ, zin, KZ)], 1)
        ok = jnp.concatenate([l // KZ == a] * 3, 1)
        shares = shares + spread(cc_ref, a, KX * KY, KZ, jnp.where(ok, m, 0.0).astype(bf16))
    shares = shares.reshape(KX, KY, 3 * LW)
    padc_v[1:1 + KX, 8:8 + KY, :] = shares[:, :, 0:LW]
    for p in range(KX):
        midc_v[1 + p, 8:8 + KY] = (
            cross(padc_v, 1 + p, (8, KY))[0] + shares[p, :, LW:2 * LW])
    for p in range(KX):
        bendc_v[p] = (cross(midc_v, 1 + p, (8, KY))[0] + shares[p, :, 2 * LW:]) * BEND

    for d in range(1, nz):
        coarse_z(d, me[2]).wait_send()
        coarse_z(d, lax.rem(me[2] + nz - d, nz)).wait_recv()
    block = cz_v[0]
    for n in range(1, nz):
        block = block + cz_v[n]

    cp_v[me[0], me[1]] = block

    def coarse_plane(ox, oy, sx, sy):
        return pltpu.make_async_remote_copy(
            src_ref=cp_v.at[sx, sy], dst_ref=cp_v.at[sx, sy],
            send_sem=ps_sem.at[ox, oy], recv_sem=pr_sem.at[ox, oy],
            device_id=in_plane(ox, oy), device_id_type=MESH)

    for ox, oy in plane:
        coarse_plane(ox, oy, me[0], me[1]).start()

    for side in SIDES:
        @pl.when(has[2][side])
        def _(side=side):
            fine_z(side).wait_send()

        @pl.when(has[2][1 - side])
        def _(side=side):
            fine_z(side).wait_recv()
    for a in range(3):
        zt_v[a * PZ:a * PZ + 2] = zg_v[0, 2 * a:2 * a + 2]
        zt_v[(a + 1) * PZ - 2:(a + 1) * PZ] = zg_v[1, 2 * a:2 * a + 2]
    g_v[...] = (part_v[...] + zt_v[...].T[0:NF]).reshape(EX, QE, LW)
    for side in SIDES:
        at = 0 if side == 0 else PX + 2
        xm_v[side] = g_v[at:at + 2, 0:PY]
    ym_v[...] = g_v[:, PY:PY + 4]

    def fine_plane(dx, dy):
        xs, ys = (0 if dx > 0 else 1), (0 if dy > 0 else 1)
        if dy == 0:
            src, dst = xm_v.at[1 - xs], xg_v.at[xs]
        elif dx == 0:
            src, dst = ym_v.at[pl.ds(2, PX)], yg_v.at[ys]
        else:
            src = ym_v.at[pl.ds(0 if dx < 0 else PX + 2, 2)]
            dst = cg_v.at[xs, ys]
        return pltpu.make_async_remote_copy(
            src_ref=src, dst_ref=dst,
            send_sem=as_sem.at[dx + 1, dy + 1], recv_sem=ar_sem.at[dx + 1, dy + 1],
            device_id={"gx": me[0] + dx, "gy": me[1] + dy}, device_id_type=MESH)

    def there(dx, dy):
        x, y = me[0] + dx, me[1] + dy
        return (x >= 0) & (x < nx) & (y >= 0) & (y < ny)

    for dx, dy in AROUND:
        @pl.when(there(dx, dy))
        def _(dx=dx, dy=dy):
            fine_plane(dx, dy).start()
    for dx, dy in AROUND:
        @pl.when(there(dx, dy))
        def _(dx=dx, dy=dy):
            fine_plane(dx, dy).wait_send()

        @pl.when(there(-dx, -dy))
        def _(dx=dx, dy=dy):
            fine_plane(dx, dy).wait_recv()

    row = iota((PY, LW), 0)
    for p in range(PX):
        out = g_v[2 + p, 0:PY]
        low, high = yg_v[0, p], yg_v[1, p]
        for side in SIDES:
            q = p if side == 0 else p - (PX - 2)
            if 0 <= q < 2:
                out = out + xg_v[side, q]
                low, high = low + cg_v[side, 0, q], high + cg_v[side, 1, q]
        fill = jnp.zeros((PY - 4, LW), f32)
        low = pltpu.roll(jnp.concatenate([low, fill], 0), PY - 2, 0)
        high = pltpu.roll(jnp.concatenate([high, fill], 0), PY - 2, 0)
        out = out + jnp.where(row < 2, low, jnp.where(row >= PY - 2, high, 0.0))
        for a in range(3):
            fo_ref[a, p] = (out if a == 0 else pltpu.roll(out, LW - a * PZ, 1))[:, 0:PZ]

    for ox, oy in plane:
        coarse_plane(ox, oy, me[0], me[1]).wait_send()
        coarse_plane(ox, oy, lax.rem(me[0] + nx - ox, nx),
                     lax.rem(me[1] + ny - oy, ny)).wait_recv()
    for p in range(KX):
        out = bendc_v[p]
        for ix in range(nx):
            q = p + 2 - ix * (SX // SPC)
            if 0 <= q < XC:
                for iy in range(ny):
                    out = out + cp_v[ix, iy, q]
        for a in range(3):
            co_ref[a, p] = (out if a == 0 else pltpu.roll(out, LW - a * KZ, 1))[:, 0:KZ]


def write_out(f_ref, c_ref, fo_ref, co_ref):
    fo_ref[...] = f_ref[...]
    co_ref[...] = c_ref[...]


def solution(mesh):
    sizes = tuple(mesh.shape[a] for a in AXES)

    def step(warped, fixed, fine, coarse):
        SX, SY, SZ = warped.shape
        PX, PY, PZ = SX // SPF, SY // SPF, SZ // SPF
        KX, KY, KZ = coarse.shape[1:]
        nx, ny, nz = sizes
        EX, QE = PX + 4, PY + 8
        XC, QC = SX // SPC + 4, KY
        KV = SPF * SY
        NF, NC, LW = EX * QE, XC * QC, 128
        vmem = pl.BlockSpec(memory_space=pltpu.VMEM)
        hbm = pl.BlockSpec(memory_space=pltpu.HBM)
        V = pltpu.VMEM
        D = pltpu.SemaphoreType.DMA
        held = pl.pallas_call(
            functools.partial(kernel, sizes),
            out_shape=(pltpu.VMEM(fine.shape, f32), pltpu.VMEM(coarse.shape, f32)),
            in_specs=[hbm] * 4,
            out_specs=(vmem, vmem),
            scratch_shapes=[
                V((SX, SY, SZ), f32), V((SX, SY, SZ), f32),
                V((3, PX, PY, PZ), f32), V(coarse.shape, f32),
                V((SX + 4, SY + 16, SZ), f32),
                V((2, 2, SX, SZ), f32), V((2, 2, SX, SZ), f32),
                V((2, SY, SZ), f32), V((2, SY, SZ), f32), V((2, SY, SZ), f32),
                V((2, 5 * QE, KV), bf16), V((SPC // SPF, 2, 4 * QC, KV), bf16),
                V((2, NF + NC, 4 * SX), bf16), V((2, QE + QC, SY), bf16),
                V((EX + XC, 2 * SZ), f32),
                V((2, 3 * SZ, 2 * LW), bf16), V((2, 2 * SZ, 2 * LW), bf16),
                V((2, KV, 3 * SZ), bf16), V((2, KV, 3 * SZ), bf16),
                V((EX, QE, 3 * SZ), f32), V((XC, QC, 3 * SZ), f32),
                V((PX + 6, PY + 16, LW), f32), V((PX + 6, PY + 16, LW), f32),
                V((EX, QE, LW), f32),
                V((KX + 2, KY + 16, LW), f32), V((KX + 2, KY + 16, LW), f32),
                V((KX, KY, LW), f32),
                V((NF, LW), f32), V((2, 8, 2 * LW), f32), V((2, 8, 2 * LW), f32),
                V((LW, 2 * LW), f32), V((EX, QE, LW), f32),
                V((2, 2, PY, LW), f32), V((EX, 4, LW), f32),
                V((2, 2, PY, LW), f32), V((2, PX, 4, LW), f32), V((2, 2, 2, 4, LW), f32),
                V((nz, XC, QC, LW), f32), V((nx, ny, XC, QC, LW), f32),
                D((2, SX // SPF)), D((2,)), D((3, 2)), D((3, 2)), D((2, 4)), D((2, 4)),
                D((2,)), D((2,)), D((3, 3)), D((3, 3)), D((nz,)), D((nz,)),
                D((nx, ny)), D((nx, ny)),
            ],
            compiler_params=pltpu.CompilerParams(
                collective_id=0, has_side_effects=True, vmem_limit_bytes=64000000
            ),
        )(warped, fixed, fine, coarse)
        held = [pltpu.with_memory_space_constraint(h, memory_space=pltpu.VMEM) for h in held]
        return pl.pallas_call(
            write_out,
            out_shape=(jax.ShapeDtypeStruct(fine.shape, f32),
                       jax.ShapeDtypeStruct(coarse.shape, f32)),
            in_specs=[vmem] * 2,
            out_specs=(vmem, vmem),
        )(*held)

    in_specs = (P("gx", "gy", "gz"), P("gx", "gy", "gz"), P(None, "gx", "gy", "gz"), P())
    out_specs = (P(None, "gx", "gy", "gz"), P())
    return jax.shard_map(
        step, mesh=mesh, in_specs=in_specs, out_specs=out_specs, check_vma=False
    )
```

time: 32.3 us -> 22.2 us (0.69)
  Pallas kernels: 31.5 us -> 21.4 us
    pallas_call x1, Pallas kernels: 30.9 us -> 20.7 us  [step(): pl.pallas_call(functools.partial(kernel, sizes), out_shape=(pltpu.VMEM(fi...]
where the time goes in v2:
time: 22.2 us; the launch traced here: 22 us
  Pallas kernels  21.4 us (96%)
  between operations  0.64 us (3%)
    pallas_call x1, Pallas kernels, step(): pl.pallas_call(functools.partial(kernel, sizes), out_shape=(pltpu.VMEM(fi...  20.7 us
    pallas_call x1, Pallas kernels, step(): pl.pallas_call(write_out, out_shape=(jax.ShapeDtypeStruct(fine.shape, f32...  0.67 us

profile of v2, /device:TPU:0, one launch (start us, length us, event | category | flops | bytes accessed | tf_op | source)
XLA Modules:
  0.0 22.0 jit_solution(11043947003830793556)
XLA Ops:
  0.6 20.7 %shard_map.59 = (f32[3,8,8,16]{3,2,1,0:T(8,128)S(1)}, f32[3,8,4,16]{3,2,1,0:T(4,128)S(1)}) custom-call(f32[64,64,128]{2,1,0:T(8,128)} %w_hbm.1, f32[64,64,128]{2,1,0:T(8,128)} %f_hbm.1, f32[3,8,8,16]{3,2,1,0:T(8,128)} %fc_hbm.1, f32[3,8,4,16]{3,2,1,0:T(4,128)} %cc_hbm.1), custom_call_target="tpu_custom_call" | custom-call | tf_op jit(solution)/shard_map/pallas_call | solution.py:607
  21.3 0.7 %shard_map.60 = (f32[3,8,8,16]{3,2,1,0:T(8,128)}, f32[3,8,4,16]{3,2,1,0:T(4,128)}) custom-call(f32[3,8,8,16]{3,2,1,0:T(8,128)S(1)} %get-tuple-element.4.f_ref, f32[3,8,4,16]{3,2,1,0:T(4,128)S(1)} %get-tuple-element.5.c_ref), custom_call_target="tpu_custom_call" | custom-call | tf_op jit(solution)/shard_map/pallas_call | solution.py:642

commit v3 on v2

--- a/solution.py
+++ b/solution.py
@@ -15,7 +15,11 @@
 bf16 = jnp.bfloat16
 AXES = ("gx", "gy", "gz")
 SIDES = (0, 1)
-AROUND = [(dx, dy) for dx in (-1, 0, 1) for dy in (-1, 0, 1) if dx or dy]
+BEFORE = 3
+STEPS = (-1, 0, 1)
+AROUND = sorted(
+    ((dx, dy, dz) for dx in STEPS for dy in STEPS for dz in STEPS if dx or dy or dz),
+    key=lambda d: -sum(map(abs, d)))
 
 
 def dot(a, b):
@@ -80,22 +84,25 @@
 def kernel(sizes, w_hbm, f_hbm, fc_hbm, cc_hbm, fo_ref, co_ref,
            w_v, f_v, fc_ref, cc_ref, s_v, ysend, yrecv, zsend, zrecv, dz_v,
            wf_v, wc_v, wy_v, wq_v, wx_v, wz_v, wh_v, fh_v, fl_v,
-           accf, accc, pad_v, mid_v, bend_v, padc_v, midc_v, bendc_v,
-           part_v, zm_v, zg_v, zt_v, g_v, xm_v, ym_v, xg_v, yg_v, cg_v,
-           cz_v, cp_v,
+           accf, accc, pad_v, mid_v, bend_v, padc_v, midc_v,
+           zm_v, zg_v, zt_v, xm_v, ym_v, xg_v, yg_v, cg_v, all_v,
            load_sem, small_sem, hs_sem, hr_sem, ys_sem, yr_sem,
-           ms_sem, mr_sem, as_sem, ar_sem, cs_sem, cr_sem, ps_sem, pr_sem):
+           as_sem, ar_sem, cs_sem, cr_sem, in_sem):
     nx, ny, nz = sizes
     me = [lax.axis_index(a) for a in AXES]
     SX, SY, SZ = w_v.shape
     PX, PY, PZ = SX // SPF, SY // SPF, SZ // SPF
     KX, KY, KZ = cc_ref.shape[1:]
     EX, QE = PX + 4, PY + 8
-    XC, QC = accc.shape[:2]
+    QC, XR = accc.shape[:2]
+    CX, CZ = SX // SPC, SZ // SPC
+    XC, ZC = CX + 4, CZ + 4
+    GL = 32
+    PG = 128 // GL
     cells = SX // SPF
     per = SPC // SPF
     lanes = 3 * SZ
-    NF, NC = EX * QE, XC * QC
+    NF, NC = EX * QE, QC * XR
     LW = 128
     has = [(me[k] > 0, me[k] < sizes[k] - 1) for k in range(3)]
 
@@ -110,10 +117,16 @@
             pltpu.make_async_copy(w_hbm.at[part], w_v.at[part], load_sem.at[0, c]),
             pltpu.make_async_copy(f_hbm.at[part], f_v.at[part], load_sem.at[1, c]),
         ))
-    order = [0, cells - 1] + list(range(1, cells - 1))
-    for c in order:
+    groups = [(0, 1), (cells - 2, cells - 1)]
+    groups += [(c, c + 1) for c in range(2, cells - 2, 2)]
+    for c in sum(groups, ()):
         loads[c][0].start()
         loads[c][1].start()
+
+    for at in (0, SX + 2):
+        s_v[at:at + 2, 8:8 + SY, :] = jnp.zeros((2, SY, SZ), f32)
+    for ref in (yrecv, zrecv, xg_v, yg_v, cg_v, zg_v):
+        ref[...] = jnp.zeros(ref.shape, f32)
 
     barrier = pltpu.get_barrier_semaphore()
     total = 0
@@ -132,39 +145,8 @@
 
     s_v[2:SX + 2, 0:8, :] = jnp.zeros((SX, 8, SZ), f32)
     s_v[2:SX + 2, 8 + SY:16 + SY, :] = jnp.zeros((SX, 8, SZ), f32)
-    accf[...] = jnp.zeros(accf.shape, f32)
-    accc[...] = jnp.zeros(accc.shape, f32)
-    pad_v[...] = jnp.zeros(pad_v.shape, f32)
-    mid_v[...] = jnp.zeros(mid_v.shape, f32)
-    padc_v[...] = jnp.zeros(padc_v.shape, f32)
-    midc_v[...] = jnp.zeros(midc_v.shape, f32)
-    zt_v[...] = jnp.zeros(zt_v.shape, f32)
-    dz_v[...] = jnp.zeros(dz_v.shape, f32)
-    zsend[...] = jnp.zeros(zsend.shape, f32)
-    xpad = (pl.ds(0, 2), pl.ds(SX + 2, 2))
-
-    def zero(ref, index):
-        ref[index] = jnp.zeros(ref.at[index].shape, f32)
-
-    for side in SIDES:
-        @pl.when(jnp.logical_not(has[0][side]))
-        def _(side=side):
-            zero(s_v, (xpad[side], slice(8, 8 + SY)))
-            zero(xg_v, side)
-            for other in SIDES:
-                zero(cg_v, (side, other))
-
-        @pl.when(jnp.logical_not(has[1][side]))
-        def _(side=side):
-            zero(yrecv, side)
-            zero(yg_v, side)
-            for other in SIDES:
-                zero(cg_v, (other, side))
-
-        @pl.when(jnp.logical_not(has[2][side]))
-        def _(side=side):
-            zero(zrecv, side)
-            zero(zg_v, side)
+    for ref in (accf, accc, pad_v, mid_v, padc_v, midc_v, zt_v, dz_v, zsend):
+        ref[...] = jnp.zeros(ref.shape, f32)
 
     def edge_row(row):
         return jnp.where(row < PY, row, jnp.where(row < PY + 2, row - PY - 2,
@@ -182,10 +164,10 @@
     for p in range(5):
         put(wf_v, (slice(p * QE, (p + 1) * QE),), along_y * along_x[p:p + 1])
     rows, cols = iota((4 * QC, KV), 0), iota((4 * QC, KV), 1)
-    along_y = weight(cols % SY + me[1] * SY, rows % QC, SPC)
+    along_y = weight(cols % SY + me[1] * SY, rows // 4, SPC)
     for ph in range(per):
         first = -2 if ph < per // 2 else -1
-        along_x = weight(cols // SY + ph * SPF, rows // QC + first, SPC)
+        along_x = weight(cols // SY + ph * SPF, rows % 4 + first, SPC)
         high, low = split2(along_x * along_y)
         wc_v[ph, 0] = high
         wc_v[ph, 1] = low
@@ -195,13 +177,14 @@
     yat = jnp.where(place < 2, place, SY - 4 + place)
     along_y = weight(yat, edge_row(iota((16, KH), 0)), SPF)
     along_x = weight(iota((16, KH), 1) % SX, iota((16, KH), 0) - 2, SPF)
-    for p in range(EX):
-        put(wy_v, (slice(p * QE, (p + 1) * QE),), along_y * along_x[p:p + 1])
+    turned = list(range(2, 2 + PX)) + [0, 1, PX + 2, PX + 3]
+    for n, p in enumerate(turned):
+        put(wy_v, (slice(n * QE, (n + 1) * QE),), along_y * along_x[p:p + 1])
     rows, cols = iota((NC, KH), 0), iota((NC, KH), 1)
     place = cols // SX
     yat = jnp.where(place < 2, place, SY - 4 + place)
-    put(wy_v, (slice(NF, NF + NC),), weight(cols % SX, rows // QC - 2, SPC)
-        * weight(yat + me[1] * SY, rows % QC, SPC))
+    put(wy_v, (slice(NF, NF + NC),), weight(cols % SX, rows % XR - 2, SPC)
+        * weight(yat + me[1] * SY, rows // XR, SPC))
 
     KP = 2 * SZ
     rows, cols = iota((QE, SY), 0), iota((QE, SY), 1)
@@ -211,7 +194,7 @@
     col = iota((EX, KP), 1)
     xat = jnp.where(col < SZ, (col + SZ - 2) % SZ, col % SZ) // 2
     wx_v[0:EX] = weight(xat, iota((EX, KP), 0) - 2, SPF)
-    wx_v[EX:EX + XC] = weight(xat[0:XC], iota((XC, KP), 0) - 2, SPC)
+    wx_v[EX:EX + XR] = weight(xat[0:XR], iota((XR, KP), 0) - 2, SPC)
 
     def fine_lane(l):
         e = (l - 3 * PZ) % 8
@@ -226,8 +209,8 @@
         z = z[:, 0:LW]
         comp, point = fine_lane(l)
         fine = weight(z, point, SPF) * (SPF ** -1.5 / 24.0)
-        ccomp = l // KZ
-        coarse = weight(z + me[2] * SZ, l % KZ, SPC) * (SPC ** -1.5 / 24.0)
+        ccomp = l // ZC
+        coarse = weight(z, l % ZC - 2, SPC) * (SPC ** -1.5 / 24.0)
         return jnp.concatenate([comp, ccomp], 1), jnp.concatenate([fine, coarse], 1)
 
     comp, value = both_levels(iota((SZ, 2 * LW), 0))
@@ -277,8 +260,9 @@
         centre = v[0]
         if 0 <= p < PX:
             centre = centre + shares[p, :, 2 * LW:3 * LW]
-        bend_v[2 + p, 0:PY] = centre * BEND
-        bend_v[2 + p, PY:2 * PY] = jnp.where(
+        at = turned.index(2 + p)
+        bend_v[at, 0:PY] = centre * BEND
+        bend_v[at, PY:2 * PY] = jnp.where(
             row < 2, v[1], jnp.where(row < 4, v[2], 0.0)) * BEND
 
     pieces = ys_sem.shape[1]
@@ -322,19 +306,19 @@
 
     tile_lane = iota((8, SZ), 1)
     srows = s_v.reshape((SX + 4) * (SY + 16), SZ)
-    drows = w_v.reshape(SX * SY, SZ)
-
-    def sums(c):
-        for copy in loads[c]:
-            copy.wait()
+    wrows, frows = w_v.reshape(SX * SY, SZ), f_v.reshape(SX * SY, SZ)
+
+    def sums(group):
+        for c in group:
+            for copy in loads[c]:
+                copy.wait()
         for y in range(0, SY, 8):
             rows = slice(y, y + 8)
             packs = [zsend[0, rows], zsend[1, rows], dz_v[0, rows], dz_v[1, rows]]
-            for x in range(c * SPF, (c + 1) * SPF):
+            for x in range(group[0] * SPF, (group[-1] + 1) * SPF):
                 w, f = w_v[x, rows], f_v[x, rows]
                 s, d = w + f, w - f
                 s_v[x + 2, 8 + y:16 + y] = s
-                w_v[x, rows] = d
                 shift = (2 * x + 2) % SZ
                 s, d = pltpu.roll(s, shift, 1), pltpu.roll(d, shift, 1)
                 low = tile_lane // 2 == (x + 1) % (SZ // 2)
@@ -354,7 +338,7 @@
     def forces(i, slot):
         for xx in range(SPF):
             x = i * SPF + xx
-            d = w_v[x]
+            d = w_v[x] - f_v[x]
             s = s_v[x + 2, 8:8 + SY, :]
             gx = (s_v[x, 8:8 + SY, :] - s_v[x + 4, 8:8 + SY, :]
                   + 8.0 * (s_v[x + 3, 8:8 + SY, :] - s_v[x + 1, 8:8 + SY, :]))
@@ -377,29 +361,28 @@
         out = both[:many] + both[many:] + dot(weights[:many], fl_v[slot])
         accf[i:i + 5] += out[:5 * QE].reshape(5, QE, lanes)
         at = k + (1 if ph >= per // 2 else 0)
-        accc[at:at + 4] += out[5 * QE:].reshape(4, QC, lanes)
-
-    summed, sent = set(), set()
-
-    def run_sums(c):
-        sums(c)
-        summed.add(c)
+        accc[:, at:at + 4] += out[5 * QE:].reshape(QC, 4, lanes)
+
+    def run_sums(group):
+        sums(group)
+        summed.append(group)
 
     def run_faces():
-        for piece in range(pieces):
-            inside = range(piece * each // SPF, (piece + 1) * each // SPF)
-            if piece not in sent and all(n in summed for n in inside):
-                sent.add(piece)
-                yfaces(piece)
-
-    for c in order[:3]:
-        run_sums(c)
+        while summed:
+            yfaces(summed.pop(0)[0] * SPF // each)
+
+    summed = []
+    for group in groups[:BEFORE]:
+        run_sums(group)
     pl.semaphore_wait(barrier, total)
+    for d in range(1, nz):
+        pl.semaphore_signal(
+            in_sem, inc=1, device_id={"gz": lax.rem(me[2] + d, nz)}, device_id_type=MESH)
     start_halo(0, 0)
     start_halo(0, 1)
     run_faces()
-    for c in order[3:]:
-        run_sums(c)
+    for group in groups[BEFORE:]:
+        run_sums(group)
         run_faces()
     start_halo(2, 0)
     start_halo(2, 1)
@@ -421,7 +404,8 @@
         g = (h0 - 8.0 * h1, h1) if side == 0 else (-h0, 8.0 * h0 - h1)
         for k in range(2):
             y = k if side == 0 else SY - 2 + k
-            adds.append(g[k] * drows[pl.ds(y, SX, stride=SY), :])
+            at = pl.ds(y, SX, stride=SY)
+            adds.append(g[k] * (wrows[at, :] - frows[at, :]))
     high, low = split2(jnp.concatenate(adds, 0))
     weights = wy_v[0]
     added = dot(weights, high) + dot(wy_v[1], high) + dot(weights, low)
@@ -434,42 +418,78 @@
                           pltpu.roll(ch, SZ - 2, 1) * dz_v[1]], 1)
     high, low = split2(fz)
     g = dot(wq_v[0], high) + dot(wq_v[1], high) + dot(wq_v[0], low)
-    blocks = [g[0:QE] * wx_v[p:p + 1] for p in range(EX)]
-    blocks += [g[QE:QE + QC] * wx_v[EX + p:EX + p + 1] for p in range(XC)]
+    blocks = [g[0:QE] * wx_v[p:p + 1] for p in turned]
+    blocks += [g[QE + q:QE + q + 1] * wx_v[EX:EX + XR] for q in range(QC)]
     hhigh, hlow = split2(jnp.concatenate(blocks, 0))
 
-    table = jnp.concatenate([accf[...].reshape(NF, lanes), accc[...].reshape(NC, lanes)], 0)
+    table = jnp.concatenate(
+        [accf[2:2 + PX].reshape(PX * QE, lanes), accf[0:2].reshape(2 * QE, lanes),
+         accf[2 + PX:].reshape(2 * QE, lanes), accc[...].reshape(NC, lanes)], 0)
     table = jnp.concatenate(
         [table[:, 0:SZ], table[:, SZ:2 * SZ] + added, table[:, 2 * SZ:]], 1)
     high, low = split2(table)
     whole = (dot(high, wz_v[0]) + dot(high, wz_v[1]) + dot(low, wz_v[0])
              + dot(hhigh, wh_v[0]) + dot(hhigh, wh_v[1]) + dot(hlow, wh_v[0]))
 
-    cz_v[me[2]] = whole[NF:NF + NC, LW:2 * LW].reshape(XC, QC, LW)
-
-    def coarse_z(d, slot):
+    pl.semaphore_wait(in_sem, nz - 1)
+
+    def coarse_copy(o, at):
         return pltpu.make_async_remote_copy(
-            src_ref=cz_v.at[slot], dst_ref=cz_v.at[slot],
-            send_sem=cs_sem.at[d], recv_sem=cr_sem.at[d],
-            device_id={"gz": lax.rem(me[2] + d, nz)}, device_id_type=MESH)
-
-    for d in range(1, nz):
-        coarse_z(d, me[2]).start()
+            src_ref=all_v.at[at], dst_ref=all_v.at[at],
+            send_sem=cs_sem.at[o], recv_sem=cr_sem.at[o],
+            device_id=tuple(lax.rem(me[k] + o[k], sizes[k]) for k in range(3)),
+            device_id_type=MESH)
+
+    everyone = [(ox, oy, oz) for ox in range(nx) for oy in range(ny) for oz in range(nz)][1:]
+    far = sorted(everyone, key=lambda o: -sum(min(o[k], sizes[k] - o[k]) for k in range(3)))
+    for v in range(0, QC, PG):
+        share = 0.0
+        for q in range(v, min(v + PG, QC)):
+            tile = whole[NF + q * XR:NF + (q + 1) * XR, LW:2 * LW]
+            share = share + (tile if q == v else pltpu.roll(tile, (q - v) * GL, 1))
+        all_v[me[0], me[1], me[2], v // PG] = share
+    for o in far:
+        coarse_copy(o, tuple(me)).start()
 
     fine = whole[0:NF, 0:LW] + bend_v[...].reshape(NF, LW)
-    part_v[...] = fine
     tall = jnp.concatenate([fine, jnp.zeros((2 * LW - NF, LW), f32)], 0).T
+    fine = fine.reshape(EX, QE, LW)
     for side in SIDES:
-        zm_v[side] = tall[3 * PZ + 8 * side:3 * PZ + 8 * side + 8]
-
-    def fine_z(side):
-        return neighbour_copy(2, side, zm_v.at[side], zg_v.at[1 - side],
-                              ms_sem.at[side], mr_sem.at[1 - side])
-
-    for side in SIDES:
-        @pl.when(has[2][side])
-        def _(side=side):
-            fine_z(side).start()
+        at = 3 * PZ + 8 * side
+        for half in range(2):
+            zm_v[side, half] = tall[at:at + 8, half * LW:(half + 1) * LW]
+        at = PX + 2 * side
+        xm_v[side] = fine[at:at + 2, 0:PY]
+    ym_v[...] = fine[:, PY:PY + 4]
+
+    def fine_copy(dx, dy, dz):
+        xs, ys, zs = (0 if d > 0 else 1 for d in (dx, dy, dz))
+        if dz:
+            src = zm_v.at[1 - zs, 1 if dx else 0]
+            dst = zg_v.at[zs, 1 - dx, 1 - dy]
+        elif dy == 0:
+            src, dst = xm_v.at[1 - xs], xg_v.at[xs]
+        elif dx == 0:
+            src, dst = ym_v.at[pl.ds(0, PX)], yg_v.at[ys]
+        else:
+            src, dst = ym_v.at[pl.ds(PX if dx < 0 else PX + 2, 2)], cg_v.at[xs, ys]
+        at = (dx + 1, dy + 1, dz + 1)
+        return pltpu.make_async_remote_copy(
+            src_ref=src, dst_ref=dst, send_sem=as_sem.at[at], recv_sem=ar_sem.at[at],
+            device_id=(me[0] + dx, me[1] + dy, me[2] + dz), device_id_type=MESH)
+
+    def there(step):
+        ok = None
+        for k in range(3):
+            if step[k]:
+                here = has[k][0 if step[k] < 0 else 1]
+                ok = here if ok is None else ok & here
+        return ok
+
+    for step in AROUND:
+        @pl.when(there(step))
+        def _(step=step):
+            fine_copy(*step).start()
 
     zin, l = iota((KZ, LW), 0), iota((KZ, LW), 1)
     shares = 0.0
@@ -484,77 +504,37 @@
         midc_v[1 + p, 8:8 + KY] = (
             cross(padc_v, 1 + p, (8, KY))[0] + shares[p, :, LW:2 * LW])
     for p in range(KX):
-        bendc_v[p] = (cross(midc_v, 1 + p, (8, KY))[0] + shares[p, :, 2 * LW:]) * BEND
-
-    for d in range(1, nz):
-        coarse_z(d, me[2]).wait_send()
-        coarse_z(d, lax.rem(me[2] + nz - d, nz)).wait_recv()
-    block = cz_v[0]
-    for n in range(1, nz):
-        block = block + cz_v[n]
-
-    cp_v[me[0], me[1]] = block
-
-    def coarse_plane(ox, oy, sx, sy):
-        return pltpu.make_async_remote_copy(
-            src_ref=cp_v.at[sx, sy], dst_ref=cp_v.at[sx, sy],
-            send_sem=ps_sem.at[ox, oy], recv_sem=pr_sem.at[ox, oy],
-            device_id=in_plane(ox, oy), device_id_type=MESH)
-
-    for ox, oy in plane:
-        coarse_plane(ox, oy, me[0], me[1]).start()
-
+        out = (cross(midc_v, 1 + p, (8, KY))[0] + shares[p, :, 2 * LW:]) * BEND
+        for a in range(3):
+            co_ref[a, p * KY:(p + 1) * KY] = (
+                out if a == 0 else pltpu.roll(out, LW - a * KZ, 1))
+
+    for step in AROUND:
+        back = tuple(-d for d in step)
+
+        @pl.when(there(back))
+        def _(step=step):
+            fine_copy(*step).wait_recv()
+    tile = iota((8, LW), 1)
+    x, y = tile // QE, tile % QE
     for side in SIDES:
-        @pl.when(has[2][side])
-        def _(side=side):
-            fine_z(side).wait_send()
-
-        @pl.when(has[2][1 - side])
-        def _(side=side):
-            fine_z(side).wait_recv()
-    for a in range(3):
-        zt_v[a * PZ:a * PZ + 2] = zg_v[0, 2 * a:2 * a + 2]
-        zt_v[(a + 1) * PZ - 2:(a + 1) * PZ] = zg_v[1, 2 * a:2 * a + 2]
-    g_v[...] = (part_v[...] + zt_v[...].T[0:NF]).reshape(EX, QE, LW)
-    for side in SIDES:
-        at = 0 if side == 0 else PX + 2
-        xm_v[side] = g_v[at:at + 2, 0:PY]
-    ym_v[...] = g_v[:, PY:PY + 4]
-
-    def fine_plane(dx, dy):
-        xs, ys = (0 if dx > 0 else 1), (0 if dy > 0 else 1)
-        if dy == 0:
-            src, dst = xm_v.at[1 - xs], xg_v.at[xs]
-        elif dx == 0:
-            src, dst = ym_v.at[pl.ds(2, PX)], yg_v.at[ys]
-        else:
-            src = ym_v.at[pl.ds(0 if dx < 0 else PX + 2, 2)]
-            dst = cg_v.at[xs, ys]
-        return pltpu.make_async_remote_copy(
-            src_ref=src, dst_ref=dst,
-            send_sem=as_sem.at[dx + 1, dy + 1], recv_sem=ar_sem.at[dx + 1, dy + 1],
-            device_id={"gx": me[0] + dx, "gy": me[1] + dy}, device_id_type=MESH)
-
-    def there(dx, dy):
-        x, y = me[0] + dx, me[1] + dy
-        return (x >= 0) & (x < nx) & (y >= 0) & (y < ny)
-
-    for dx, dy in AROUND:
-        @pl.when(there(dx, dy))
-        def _(dx=dx, dy=dy):
-            fine_plane(dx, dy).start()
-    for dx, dy in AROUND:
-        @pl.when(there(dx, dy))
-        def _(dx=dx, dy=dy):
-            fine_plane(dx, dy).wait_send()
-
-        @pl.when(there(-dx, -dy))
-        def _(dx=dx, dy=dy):
-            fine_plane(dx, dy).wait_recv()
-
+        got = 0.0
+        for sx in STEPS:
+            shift = {-1: -2 * QE, 0: 0, 1: (PX - 2) * QE}[sx]
+            xin = {-1: x < 2, 0: x < PX, 1: x >= PX - 2}[sx]
+            for sy in STEPS:
+                yin = {-1: y < 2, 0: y < PY, 1: (y >= PY - 2) & (y < PY)}[sy]
+                turn = (shift + {-1: -PY - 2, 0: 0, 1: -2}[sy]) % LW
+                value = zg_v[side, 1 + sx, 1 + sy]
+                value = pltpu.roll(value, turn, 1) if turn else value
+                got = got + jnp.where(xin & yin, value, 0.0)
+        for a in range(3):
+            at = a * PZ + side * (PZ - 2)
+            zt_v[at:at + 2] = got[2 * a:2 * a + 2]
+    across = zt_v[...].T.reshape(PX, QE, LW)
     row = iota((PY, LW), 0)
     for p in range(PX):
-        out = g_v[2 + p, 0:PY]
+        out = fine[p, 0:PY] + across[p, 0:PY]
         low, high = yg_v[0, p], yg_v[1, p]
         for side in SIDES:
             q = p if side == 0 else p - (PX - 2)
@@ -568,24 +548,50 @@
         for a in range(3):
             fo_ref[a, p] = (out if a == 0 else pltpu.roll(out, LW - a * PZ, 1))[:, 0:PZ]
 
-    for ox, oy in plane:
-        coarse_plane(ox, oy, me[0], me[1]).wait_send()
-        coarse_plane(ox, oy, lax.rem(me[0] + nx - ox, nx),
-                     lax.rem(me[1] + ny - oy, ny)).wait_recv()
-    for p in range(KX):
-        out = bendc_v[p]
-        for ix in range(nx):
-            q = p + 2 - ix * (SX // SPC)
-            if 0 <= q < XC:
-                for iy in range(ny):
-                    out = out + cp_v[ix, iy, q]
-        for a in range(3):
-            co_ref[a, p] = (out if a == 0 else pltpu.roll(out, LW - a * KZ, 1))[:, 0:KZ]
+    for o in far:
+        coarse_copy(o, tuple(lax.rem(me[k] + sizes[k] - o[k], sizes[k])
+                             for k in range(3))).wait_recv()
+    row = iota((XR, LW), 0)
+    for v in range(0, QC, PG):
+        for b in range(0, KX, XR):
+            placed = []
+            for iz in range(nz):
+                here = 0.0
+                for ix in range(nx):
+                    first = CX * ix - 2 - b
+                    if first <= -XC or first >= XR:
+                        continue
+                    block = all_v[ix, 0, iz, v // PG]
+                    for iy in range(1, ny):
+                        block = block + all_v[ix, iy, iz, v // PG]
+                    block = pltpu.roll(block, first % XR, 0)
+                    here = here + jnp.where((row >= first) & (row < first + XC), block, 0.0)
+                placed.append(here)
+            for q in range(v, min(v + PG, QC)):
+                for a in range(3):
+                    out = 0.0
+                    for iz in range(nz):
+                        first = CZ * iz - 2
+                        value = pltpu.roll(placed[iz], (first - (q - v) * GL - a * ZC) % LW, 1)
+                        inside = (tile >= first) & (tile < first + ZC)
+                        out = out + jnp.where(inside, value, 0.0)
+                    at = pl.ds(b * KY + q, XR, stride=KY)
+                    co_ref[a, at, :] = co_ref[a, at, :] + out
+
+    for o in far:
+        coarse_copy(o, tuple(me)).wait_send()
+    for step in AROUND:
+        @pl.when(there(step))
+        def _(step=step):
+            fine_copy(*step).wait_send()
 
 
 def write_out(f_ref, c_ref, fo_ref, co_ref):
     fo_ref[...] = f_ref[...]
-    co_ref[...] = c_ref[...]
+    KX, KY, KZ = co_ref.shape[1:]
+    for a in range(3):
+        for p in range(KX):
+            co_ref[a, p] = c_ref[a, p * KY:(p + 1) * KY, 0:KZ]
 
 
 def solution(mesh):
@@ -597,16 +603,16 @@
         KX, KY, KZ = coarse.shape[1:]
         nx, ny, nz = sizes
         EX, QE = PX + 4, PY + 8
-        XC, QC = SX // SPC + 4, KY
+        XR, QC = -(-(SX // SPC + 4) // 8) * 8, KY
         KV = SPF * SY
-        NF, NC, LW = EX * QE, XC * QC, 128
+        NF, NC, LW = EX * QE, XR * QC, 128
         vmem = pl.BlockSpec(memory_space=pltpu.VMEM)
         hbm = pl.BlockSpec(memory_space=pltpu.HBM)
         V = pltpu.VMEM
         D = pltpu.SemaphoreType.DMA
         held = pl.pallas_call(
             functools.partial(kernel, sizes),
-            out_shape=(pltpu.VMEM(fine.shape, f32), pltpu.VMEM(coarse.shape, f32)),
+            out_shape=(pltpu.VMEM(fine.shape, f32), pltpu.VMEM((3, KX * KY, LW), f32)),
             in_specs=[hbm] * 4,
             out_specs=(vmem, vmem),
             scratch_shapes=[
@@ -617,22 +623,19 @@
                 V((2, SY, SZ), f32), V((2, SY, SZ), f32), V((2, SY, SZ), f32),
                 V((2, 5 * QE, KV), bf16), V((SPC // SPF, 2, 4 * QC, KV), bf16),
                 V((2, NF + NC, 4 * SX), bf16), V((2, QE + QC, SY), bf16),
-                V((EX + XC, 2 * SZ), f32),
+                V((EX + XR, 2 * SZ), f32),
                 V((2, 3 * SZ, 2 * LW), bf16), V((2, 2 * SZ, 2 * LW), bf16),
                 V((2, KV, 3 * SZ), bf16), V((2, KV, 3 * SZ), bf16),
-                V((EX, QE, 3 * SZ), f32), V((XC, QC, 3 * SZ), f32),
+                V((EX, QE, 3 * SZ), f32), V((QC, XR, 3 * SZ), f32),
                 V((PX + 6, PY + 16, LW), f32), V((PX + 6, PY + 16, LW), f32),
                 V((EX, QE, LW), f32),
                 V((KX + 2, KY + 16, LW), f32), V((KX + 2, KY + 16, LW), f32),
-                V((KX, KY, LW), f32),
-                V((NF, LW), f32), V((2, 8, 2 * LW), f32), V((2, 8, 2 * LW), f32),
-                V((LW, 2 * LW), f32), V((EX, QE, LW), f32),
+                V((2, 2, 8, LW), f32), V((2, 3, 3, 8, LW), f32), V((LW, LW), f32),
                 V((2, 2, PY, LW), f32), V((EX, 4, LW), f32),
                 V((2, 2, PY, LW), f32), V((2, PX, 4, LW), f32), V((2, 2, 2, 4, LW), f32),
-                V((nz, XC, QC, LW), f32), V((nx, ny, XC, QC, LW), f32),
+                V((nx, ny, nz, -(-QC // 4), XR, LW), f32),
                 D((2, SX // SPF)), D((2,)), D((3, 2)), D((3, 2)), D((2, 4)), D((2, 4)),
-                D((2,)), D((2,)), D((3, 3)), D((3, 3)), D((nz,)), D((nz,)),
-                D((nx, ny)), D((nx, ny)),
+                D((3, 3, 3)), D((3, 3, 3)), D(sizes), D(sizes), pltpu.SemaphoreType.REGULAR,
             ],
             compiler_params=pltpu.CompilerParams(
                 collective_id=0, has_side_effects=True, vmem_limit_bytes=64000000

time: 22.2 us -> 21.1 us (0.950)
  Pallas kernels: 21.4 us -> 20.3 us
    pallas_call x1, Pallas kernels: 20.7 us -> 19.6 us  [step(): pl.pallas_call(functools.partial(kernel, sizes), out_shape=(pltpu.VMEM(fi...]
where the time goes in v3:
time: 21.1 us; the launch traced here: 20.9 us
  Pallas kernels  20.3 us (96%)
  between operations  0.64 us (3%)
    pallas_call x1, Pallas kernels, step(): pl.pallas_call(functools.partial(kernel, sizes), out_shape=(pltpu.VMEM(fi...  19.6 us
    pallas_call x1, Pallas kernels, step(): pl.pallas_call(write_out, out_shape=(jax.ShapeDtypeStruct(fine.shape, f32...  0.67 us

profile of v3, /device:TPU:0, one launch (start us, length us, event | category | flops | bytes accessed | tf_op | source)
XLA Modules:
  0.0 20.9 jit_solution(15080552187330538042)
XLA Ops:
  0.6 19.6 %shard_map.59 = (f32[3,8,8,16]{3,2,1,0:T(8,128)S(1)}, f32[3,32,128]{2,1,0:T(8,128)S(1)}) custom-call(f32[64,64,128]{2,1,0:T(8,128)} %w_hbm.1, f32[64,64,128]{2,1,0:T(8,128)} %f_hbm.1, f32[3,8,8,16]{3,2,1,0:T(8,128)} %fc_hbm.1, f32[3,8,4,16]{3,2,1,0:T(4,128)} %cc_hbm.1), custom_call_target="tpu_custom_call" | custom-call | tf_op jit(solution)/shard_map/pallas_call | solution.py:613
  20.2 0.7 %shard_map.60 = (f32[3,8,8,16]{3,2,1,0:T(8,128)}, f32[3,8,4,16]{3,2,1,0:T(4,128)}) custom-call(f32[3,8,8,16]{3,2,1,0:T(8,128)S(1)} %get-tuple-element.4.f_ref, f32[3,32,128]{2,1,0:T(8,128)S(1)} %get-tuple-element.5.c_ref), custom_call_target="tpu_custom_call" | custom-call | tf_op jit(solution)/shard_map/pallas_call | solution.py:645

commit v4 on v3

--- a/solution.py
+++ b/solution.py
@@ -83,8 +83,8 @@
 
 def kernel(sizes, w_hbm, f_hbm, fc_hbm, cc_hbm, fo_ref, co_ref,
            w_v, f_v, fc_ref, cc_ref, s_v, ysend, yrecv, zsend, zrecv, dz_v,
-           wf_v, wc_v, wy_v, wq_v, wx_v, wz_v, wh_v, fh_v, fl_v,
-           accf, accc, pad_v, mid_v, bend_v, padc_v, midc_v,
+           wf_v, wc_v, wy_v, wq_v, wx_v, wz_v, wh_v, fh_v, fl_v, parts_v, band_v,
+           accf, accc, whole_v, pad_v, mid_v, bend_v, padc_v, midc_v,
            zm_v, zg_v, zt_v, xm_v, ym_v, xg_v, yg_v, cg_v, all_v,
            load_sem, small_sem, hs_sem, hr_sem, ys_sem, yr_sem,
            as_sem, ar_sem, cs_sem, cr_sem, in_sem):
@@ -228,6 +228,12 @@
         part = slice(side * SZ, (side + 1) * SZ)
         put(wh_v, (part,), jnp.where(odd, value[2 * side + 1:2 * side + 2],
                                      value[2 * side:2 * side + 1]))
+
+    step = iota((SZ, SZ), 1) - iota((SZ, SZ), 0)
+    band = (jnp.where(step == 2, 1.0, 0.0) - jnp.where(step == 1, 8.0, 0.0)
+            + jnp.where(step == -1, 8.0, 0.0) - jnp.where(step == -2, 1.0, 0.0)).astype(bf16)
+    band_v[0:SZ] = band
+    band_v[SZ:2 * SZ] = band
 
     for copy in small:
         copy.wait()
@@ -304,7 +310,13 @@
                 def _(side=side, piece=piece):
                     halo(k, side, piece).wait_recv()
 
-    tile_lane = iota((8, SZ), 1)
+    tile_lane = iota((16, SZ), 1)
+
+    def pack(packs, value, x):
+        value = pltpu.roll(value, (2 * x + 2) % SZ, 1)
+        low = tile_lane // 2 == (x + 1) % (SZ // 2)
+        return [jnp.where(low, value, packs[0]), jnp.where(tile_lane // 2 == x, value, packs[1])]
+
     srows = s_v.reshape((SX + 4) * (SY + 16), SZ)
     wrows, frows = w_v.reshape(SX * SY, SZ), f_v.reshape(SX * SY, SZ)
 
@@ -312,20 +324,17 @@
         for c in group:
             for copy in loads[c]:
                 copy.wait()
-        for y in range(0, SY, 8):
-            rows = slice(y, y + 8)
-            packs = [zsend[0, rows], zsend[1, rows], dz_v[0, rows], dz_v[1, rows]]
+        for y in range(0, SY, 16):
+            rows = slice(y, y + 16)
+            packs = [zsend[0, rows], zsend[1, rows]]
             for x in range(group[0] * SPF, (group[-1] + 1) * SPF):
-                w, f = w_v[x, rows], f_v[x, rows]
-                s, d = w + f, w - f
-                s_v[x + 2, 8 + y:16 + y] = s
-                shift = (2 * x + 2) % SZ
-                s, d = pltpu.roll(s, shift, 1), pltpu.roll(d, shift, 1)
-                low = tile_lane // 2 == (x + 1) % (SZ // 2)
-                high = tile_lane // 2 == x
-                packs = [jnp.where(low, s, packs[0]), jnp.where(high, s, packs[1]),
-                         jnp.where(low, d, packs[2]), jnp.where(high, d, packs[3])]
-            zsend[0, rows], zsend[1, rows], dz_v[0, rows], dz_v[1, rows] = packs
+                s = w_v[x, rows] + f_v[x, rows]
+                s_v[x + 2, 8 + y:24 + y] = s
+                high, low = split2(s)
+                parts_v[x * SY + y:x * SY + y + 16, 0:SZ] = high
+                parts_v[x * SY + y:x * SY + y + 16, SZ:2 * SZ] = low
+                packs = pack(packs, s, x)
+            zsend[0, rows], zsend[1, rows] = packs
 
     def yfaces(piece):
         for side in SIDES:
@@ -336,20 +345,24 @@
             start_halo(1, side, piece)
 
     def forces(i, slot):
-        for xx in range(SPF):
-            x = i * SPF + xx
-            d = w_v[x] - f_v[x]
-            s = s_v[x + 2, 8:8 + SY, :]
-            gx = (s_v[x, 8:8 + SY, :] - s_v[x + 4, 8:8 + SY, :]
-                  + 8.0 * (s_v[x + 3, 8:8 + SY, :] - s_v[x + 1, 8:8 + SY, :]))
-            gy = (s_v[x + 2, 6:6 + SY, :] - s_v[x + 2, 10:10 + SY, :]
-                  + 8.0 * (s_v[x + 2, 9:9 + SY, :] - s_v[x + 2, 7:7 + SY, :]))
-            gz = (pltpu.roll(s, 2, 1) - pltpu.roll(s, SZ - 2, 1)
-                  + 8.0 * (pltpu.roll(s, SZ - 1, 1) - pltpu.roll(s, 1, 1)))
-            for a, g in enumerate((gx, gy, gz)):
-                high, low = split2(g * d)
-                fh_v[slot, xx * SY:(xx + 1) * SY, a * SZ:(a + 1) * SZ] = high
-                fl_v[slot, xx * SY:(xx + 1) * SY, a * SZ:(a + 1) * SZ] = low
+        slopes = dot(parts_v[i * KV:(i + 1) * KV], band_v[...])
+        for y in range(0, SY, 16):
+            rows = slice(8 + y, 24 + y)
+            slabs = [s_v[i * SPF + x, rows] for x in range(SPF + 4)]
+            packs = [dz_v[0, y:y + 16], dz_v[1, y:y + 16]]
+            for xx in range(SPF):
+                x = i * SPF + xx
+                d = w_v[x, y:y + 16] - f_v[x, y:y + 16]
+                packs = pack(packs, d, x)
+                gx = slabs[xx] - slabs[xx + 4] + 8.0 * (slabs[xx + 3] - slabs[xx + 1])
+                gy = (s_v[x + 2, 6 + y:22 + y] - s_v[x + 2, 10 + y:26 + y]
+                      + 8.0 * (s_v[x + 2, 9 + y:25 + y] - s_v[x + 2, 7 + y:23 + y]))
+                gz = slopes[xx * SY + y:xx * SY + y + 16]
+                for a, g in enumerate((gx, gy, gz)):
+                    at = (slot, slice(xx * SY + y, xx * SY + y + 16),
+                          slice(a * SZ, (a + 1) * SZ))
+                    fh_v[at], fl_v[at] = split2(g * d)
+            dz_v[0, y:y + 16], dz_v[1, y:y + 16] = packs
 
     lane = iota((SY, SZ), 1)
 
@@ -396,6 +409,13 @@
             forces(turn[n + 1], (n + 1) % 2)
         gather(i, n % 2)
 
+    table = jnp.concatenate(
+        [accf[2:2 + PX].reshape(PX * QE, lanes), accf[0:2].reshape(2 * QE, lanes),
+         accf[2 + PX:].reshape(2 * QE, lanes), accc[...].reshape(NC, lanes)], 0)
+    high, low = split2(table)
+    whole_v[...] = dot(high, wz_v[0]) + dot(high, wz_v[1]) + dot(low, wz_v[0])
+    whole_v[0:NF, 0:LW] = whole_v[0:NF, 0:LW] + bend_v[...].reshape(NF, LW)
+
     wait_halo(1)
     wait_halo(2)
     adds = []
@@ -411,7 +431,7 @@
     added = dot(weights, high) + dot(wy_v[1], high) + dot(weights, low)
 
     even = lane % 2 == 0
-    hl, hh = zrecv[0] - zsend[1], zrecv[1] - zsend[0]
+    hl, hh = zrecv[0], zrecv[1]
     cl = jnp.where(even, hl - 8.0 * pltpu.roll(hl, SZ - 1, 1), hl)
     ch = jnp.where(even, -hh, 8.0 * pltpu.roll(hh, 1, 1) - hh)
     fz = jnp.concatenate([pltpu.roll(cl, 2, 1) * dz_v[0],
@@ -422,21 +442,25 @@
     blocks += [g[QE + q:QE + q + 1] * wx_v[EX:EX + XR] for q in range(QC)]
     hhigh, hlow = split2(jnp.concatenate(blocks, 0))
 
-    table = jnp.concatenate(
-        [accf[2:2 + PX].reshape(PX * QE, lanes), accf[0:2].reshape(2 * QE, lanes),
-         accf[2 + PX:].reshape(2 * QE, lanes), accc[...].reshape(NC, lanes)], 0)
-    table = jnp.concatenate(
-        [table[:, 0:SZ], table[:, SZ:2 * SZ] + added, table[:, 2 * SZ:]], 1)
-    high, low = split2(table)
-    whole = (dot(high, wz_v[0]) + dot(high, wz_v[1]) + dot(low, wz_v[0])
-             + dot(hhigh, wh_v[0]) + dot(hhigh, wh_v[1]) + dot(hlow, wh_v[0]))
+    high, low = split2(added)
+    part = slice(SZ, 2 * SZ)
+    whole = whole_v[...] + (
+        dot(high, wz_v[0, part]) + dot(high, wz_v[1, part]) + dot(low, wz_v[0, part])
+        + dot(hhigh, wh_v[0]) + dot(hhigh, wh_v[1]) + dot(hlow, wh_v[0]))
 
     pl.semaphore_wait(in_sem, nz - 1)
+
+    mine = (me[0] * ny + me[1]) * nz + me[2]
+    count = nx * ny * nz - 1
+
+    def coarse_wait(sem):
+        ref = all_v.at[pl.ds(0, count)]
+        pltpu.make_async_copy(ref, ref, sem).wait()
 
     def coarse_copy(o, at):
         return pltpu.make_async_remote_copy(
             src_ref=all_v.at[at], dst_ref=all_v.at[at],
-            send_sem=cs_sem.at[o], recv_sem=cr_sem.at[o],
+            send_sem=cs_sem, recv_sem=cr_sem,
             device_id=tuple(lax.rem(me[k] + o[k], sizes[k]) for k in range(3)),
             device_id_type=MESH)
 
@@ -447,11 +471,11 @@
         for q in range(v, min(v + PG, QC)):
             tile = whole[NF + q * XR:NF + (q + 1) * XR, LW:2 * LW]
             share = share + (tile if q == v else pltpu.roll(tile, (q - v) * GL, 1))
-        all_v[me[0], me[1], me[2], v // PG] = share
+        all_v[mine, v // PG] = share[0:XC]
     for o in far:
-        coarse_copy(o, tuple(me)).start()
-
-    fine = whole[0:NF, 0:LW] + bend_v[...].reshape(NF, LW)
+        coarse_copy(o, mine).start()
+
+    fine = whole[0:NF, 0:LW]
     tall = jnp.concatenate([fine, jnp.zeros((2 * LW - NF, LW), f32)], 0).T
     fine = fine.reshape(EX, QE, LW)
     for side in SIDES:
@@ -548,9 +572,13 @@
         for a in range(3):
             fo_ref[a, p] = (out if a == 0 else pltpu.roll(out, LW - a * PZ, 1))[:, 0:PZ]
 
-    for o in far:
-        coarse_copy(o, tuple(lax.rem(me[k] + sizes[k] - o[k], sizes[k])
-                             for k in range(3))).wait_recv()
+    for step in AROUND:
+        @pl.when(there(step))
+        def _(step=step):
+            fine_copy(*step).wait_send()
+    if count:
+        coarse_wait(cs_sem)
+        coarse_wait(cr_sem)
     row = iota((XR, LW), 0)
     for v in range(0, QC, PG):
         for b in range(0, KX, XR):
@@ -561,9 +589,10 @@
                     first = CX * ix - 2 - b
                     if first <= -XC or first >= XR:
                         continue
-                    block = all_v[ix, 0, iz, v // PG]
+                    block = all_v[ix * ny * nz + iz, v // PG]
                     for iy in range(1, ny):
-                        block = block + all_v[ix, iy, iz, v // PG]
+                        block = block + all_v[(ix * ny + iy) * nz + iz, v // PG]
+                    block = jnp.concatenate([block, jnp.zeros((XR - XC, LW), f32)], 0)
                     block = pltpu.roll(block, first % XR, 0)
                     here = here + jnp.where((row >= first) & (row < first + XC), block, 0.0)
                 placed.append(here)
@@ -577,13 +606,6 @@
                         out = out + jnp.where(inside, value, 0.0)
                     at = pl.ds(b * KY + q, XR, stride=KY)
                     co_ref[a, at, :] = co_ref[a, at, :] + out
-
-    for o in far:
-        coarse_copy(o, tuple(me)).wait_send()
-    for step in AROUND:
-        @pl.when(there(step))
-        def _(step=step):
-            fine_copy(*step).wait_send()
 
 
 def write_out(f_ref, c_ref, fo_ref, co_ref):
@@ -626,16 +648,18 @@
                 V((EX + XR, 2 * SZ), f32),
                 V((2, 3 * SZ, 2 * LW), bf16), V((2, 2 * SZ, 2 * LW), bf16),
                 V((2, KV, 3 * SZ), bf16), V((2, KV, 3 * SZ), bf16),
+                V((SX * SY, 2 * SZ), bf16), V((2 * SZ, SZ), bf16),
                 V((EX, QE, 3 * SZ), f32), V((QC, XR, 3 * SZ), f32),
+                V((NF + NC, 2 * LW), f32),
                 V((PX + 6, PY + 16, LW), f32), V((PX + 6, PY + 16, LW), f32),
                 V((EX, QE, LW), f32),
                 V((KX + 2, KY + 16, LW), f32), V((KX + 2, KY + 16, LW), f32),
                 V((2, 2, 8, LW), f32), V((2, 3, 3, 8, LW), f32), V((LW, LW), f32),
                 V((2, 2, PY, LW), f32), V((EX, 4, LW), f32),
                 V((2, 2, PY, LW), f32), V((2, PX, 4, LW), f32), V((2, 2, 2, 4, LW), f32),
-                V((nx, ny, nz, -(-QC // 4), XR, LW), f32),
+                V((nx * ny * nz, -(-QC // 4), SX // SPC + 4, LW), f32),
                 D((2, SX // SPF)), D((2,)), D((3, 2)), D((3, 2)), D((2, 4)), D((2, 4)),
-                D((3, 3, 3)), D((3, 3, 3)), D(sizes), D(sizes), pltpu.SemaphoreType.REGULAR,
+                D((3, 3, 3)), D((3, 3, 3)), D(()), D(()), pltpu.SemaphoreType.REGULAR,
             ],
             compiler_params=pltpu.CompilerParams(
                 collective_id=0, has_side_effects=True, vmem_limit_bytes=64000000

time: 21.1 us -> 19.5 us (0.924)
  Pallas kernels: 20.3 us -> 18.7 us
    pallas_call x1, Pallas kernels: 19.6 us -> 18 us  [step(): pl.pallas_call(functools.partial(kernel, sizes), out_shape=(pltpu.VMEM(fi...]
where the time goes in v4:
time: 19.5 us; the launch traced here: 19.3 us
  Pallas kernels  18.7 us (96%)
  between operations  0.64 us (3%)
    pallas_call x1, Pallas kernels, step(): pl.pallas_call(functools.partial(kernel, sizes), out_shape=(pltpu.VMEM(fi...  18 us
    pallas_call x1, Pallas kernels, step(): pl.pallas_call(write_out, out_shape=(jax.ShapeDtypeStruct(fine.shape, f32...  0.67 us

profile of v4, /device:TPU:0, one launch (start us, length us, event | category | flops | bytes accessed | tf_op | source)
XLA Modules:
  0.0 19.3 jit_solution(12654089237363387968)
XLA Ops:
  0.6 18.0 %shard_map.59 = (f32[3,8,8,16]{3,2,1,0:T(8,128)S(1)}, f32[3,32,128]{2,1,0:T(8,128)S(1)}) custom-call(f32[64,64,128]{2,1,0:T(8,128)} %w_hbm.1, f32[64,64,128]{2,1,0:T(8,128)} %f_hbm.1, f32[3,8,8,16]{3,2,1,0:T(8,128)} %fc_hbm.1, f32[3,8,4,16]{3,2,1,0:T(4,128)} %cc_hbm.1), custom_call_target="tpu_custom_call" | custom-call | tf_op jit(solution)/shard_map/pallas_call | solution.py:635
  18.7 0.7 %shard_map.60 = (f32[3,8,8,16]{3,2,1,0:T(8,128)}, f32[3,8,4,16]{3,2,1,0:T(4,128)}) custom-call(f32[3,8,8,16]{3,2,1,0:T(8,128)S(1)} %get-tuple-element.4.f_ref, f32[3,32,128]{2,1,0:T(8,128)S(1)} %get-tuple-element.5.c_ref), custom_call_target="tpu_custom_call" | custom-call | tf_op jit(solution)/shard_map/pallas_call | solution.py:669

commit v5 on v4

--- a/solution.py
+++ b/solution.py
@@ -15,7 +15,7 @@
 bf16 = jnp.bfloat16
 AXES = ("gx", "gy", "gz")
 SIDES = (0, 1)
-BEFORE = 3
+BEFORE = 2
 STEPS = (-1, 0, 1)
 AROUND = sorted(
     ((dx, dy, dz) for dx in STEPS for dy in STEPS for dz in STEPS if dx or dy or dz),
@@ -171,6 +171,137 @@
         high, low = split2(along_x * along_y)
         wc_v[ph, 0] = high
         wc_v[ph, 1] = low
+
+    pieces = ys_sem.shape[1]
+    each = SX // pieces
+
+    def neighbour_copy(k, side, src, dst, send, recv):
+        other = me[k] - 1 if side == 0 else me[k] + 1
+        return pltpu.make_async_remote_copy(
+            src_ref=src, dst_ref=dst, send_sem=send, recv_sem=recv,
+            device_id={AXES[k]: other}, device_id_type=MESH,
+        )
+
+    def halo(k, side, piece=0):
+        if k == 1:
+            part = pl.ds(piece * each, each)
+            return neighbour_copy(
+                k, side, ysend.at[side, :, part], yrecv.at[1 - side, :, part],
+                ys_sem.at[side, piece], yr_sem.at[1 - side, piece])
+        if k == 0:
+            src = s_v.at[pl.ds(2 if side == 0 else SX, 2), pl.ds(8, SY), :]
+            dst = s_v.at[pl.ds(SX + 2 if side == 0 else 0, 2), pl.ds(8, SY), :]
+        else:
+            src, dst = zsend.at[side], zrecv.at[1 - side]
+        return neighbour_copy(k, side, src, dst, hs_sem.at[k, side], hr_sem.at[k, 1 - side])
+
+    def start_halo(k, side, piece=0):
+        @pl.when(has[k][side])
+        def _():
+            halo(k, side, piece).start()
+
+    def wait_halo(k):
+        for side in SIDES:
+            for piece in range(pieces if k == 1 else 1):
+                @pl.when(has[k][side])
+                def _(side=side, piece=piece):
+                    halo(k, side, piece).wait_send()
+
+                @pl.when(has[k][1 - side])
+                def _(side=side, piece=piece):
+                    halo(k, side, piece).wait_recv()
+
+    tile_lane = iota((16, SZ), 1)
+
+    def pack(packs, value, x):
+        value = pltpu.roll(value, (2 * x + 2) % SZ, 1)
+        low = tile_lane // 2 == (x + 1) % (SZ // 2)
+        return [jnp.where(low, value, packs[0]), jnp.where(tile_lane // 2 == x, value, packs[1])]
+
+    srows = s_v.reshape((SX + 4) * (SY + 16), SZ)
+    drows = w_v.reshape(SX * SY, SZ)
+
+    def sums(group):
+        for c in group:
+            for copy in loads[c]:
+                copy.wait()
+        for y in range(0, SY, 16):
+            rows = slice(y, y + 16)
+            packs = [zsend[0, rows], zsend[1, rows]]
+            for x in range(group[0] * SPF, (group[-1] + 1) * SPF):
+                w, f = w_v[x, rows], f_v[x, rows]
+                s = w + f
+                w_v[x, rows] = w - f
+                s_v[x + 2, 8 + y:24 + y] = s
+                high, low = split2(s)
+                parts_v[x * SY + y:x * SY + y + 16, 0:SZ] = high
+                parts_v[x * SY + y:x * SY + y + 16, SZ:2 * SZ] = low
+                packs = pack(packs, s, x)
+            zsend[0, rows], zsend[1, rows] = packs
+
+    def yfaces(piece):
+        for side in SIDES:
+            for k in range(2):
+                y = k if side == 0 else SY - 2 + k
+                ysend[side, k, pl.ds(piece * each, each)] = srows[
+                    pl.ds((piece * each + 2) * (SY + 16) + 8 + y, each, stride=SY + 16), :]
+            start_halo(1, side, piece)
+
+    def forces(i, slot):
+        slopes = dot(parts_v[i * KV:(i + 1) * KV], band_v[...])
+        for y in range(0, SY, 16):
+            rows = slice(8 + y, 24 + y)
+            slabs = [s_v[i * SPF + x, rows] for x in range(SPF + 4)]
+            packs = [dz_v[0, y:y + 16], dz_v[1, y:y + 16]]
+            for xx in range(SPF):
+                x = i * SPF + xx
+                d = w_v[x, y:y + 16]
+                packs = pack(packs, d, x)
+                gx = slabs[xx] - slabs[xx + 4] + 8.0 * (slabs[xx + 3] - slabs[xx + 1])
+                gy = (s_v[x + 2, 6 + y:22 + y] - s_v[x + 2, 10 + y:26 + y]
+                      + 8.0 * (s_v[x + 2, 9 + y:25 + y] - s_v[x + 2, 7 + y:23 + y]))
+                gz = slopes[xx * SY + y:xx * SY + y + 16]
+                for a, g in enumerate((gx, gy, gz)):
+                    at = (slot, slice(xx * SY + y, xx * SY + y + 16),
+                          slice(a * SZ, (a + 1) * SZ))
+                    fh_v[at], fl_v[at] = split2(g * d)
+            dz_v[0, y:y + 16], dz_v[1, y:y + 16] = packs
+
+    lane = iota((SY, SZ), 1)
+
+    def gather(i, slot):
+        k, ph = divmod(i, per)
+        many = 5 * QE + 4 * QC
+        weights = jnp.concatenate([wf_v[0], wc_v[ph, 0], wf_v[1], wc_v[ph, 1]], axis=0)
+        both = dot(weights, fh_v[slot])
+        out = both[:many] + both[many:] + dot(weights[:many], fl_v[slot])
+        accf[i:i + 5] += out[:5 * QE].reshape(5, QE, lanes)
+        at = k + (1 if ph >= per // 2 else 0)
+        accc[:, at:at + 4] += out[5 * QE:].reshape(QC, 4, lanes)
+
+    def run_sums(group):
+        sums(group)
+        summed.append(group)
+
+    def run_faces():
+        while summed:
+            yfaces(summed.pop(0)[0] * SPF // each)
+
+    summed = []
+    for group in groups[:BEFORE]:
+        run_sums(group)
+    pl.semaphore_wait(barrier, total)
+    for d in range(1, nz):
+        pl.semaphore_signal(
+            in_sem, inc=1, device_id={"gz": lax.rem(me[2] + d, nz)}, device_id_type=MESH)
+    start_halo(0, 0)
+    start_halo(0, 1)
+    run_faces()
+    for group in groups[BEFORE:]:
+        run_sums(group)
+        run_faces()
+    start_halo(2, 0)
+    start_halo(2, 1)
 
     KH = 4 * SX
     place = (iota((16, KH), 1) // SX)
@@ -271,135 +402,6 @@
         bend_v[at, PY:2 * PY] = jnp.where(
             row < 2, v[1], jnp.where(row < 4, v[2], 0.0)) * BEND
 
-    pieces = ys_sem.shape[1]
-    each = SX // pieces
-
-    def neighbour_copy(k, side, src, dst, send, recv):
-        other = me[k] - 1 if side == 0 else me[k] + 1
-        return pltpu.make_async_remote_copy(
-            src_ref=src, dst_ref=dst, send_sem=send, recv_sem=recv,
-            device_id={AXES[k]: other}, device_id_type=MESH,
-        )
-
-    def halo(k, side, piece=0):
-        if k == 1:
-            part = pl.ds(piece * each, each)
-            return neighbour_copy(
-                k, side, ysend.at[side, :, part], yrecv.at[1 - side, :, part],
-                ys_sem.at[side, piece], yr_sem.at[1 - side, piece])
-        if k == 0:
-            src = s_v.at[pl.ds(2 if side == 0 else SX, 2), pl.ds(8, SY), :]
-            dst = s_v.at[pl.ds(SX + 2 if side == 0 else 0, 2), pl.ds(8, SY), :]
-        else:
-            src, dst = zsend.at[side], zrecv.at[1 - side]
-        return neighbour_copy(k, side, src, dst, hs_sem.at[k, side], hr_sem.at[k, 1 - side])
-
-    def start_halo(k, side, piece=0):
-        @pl.when(has[k][side])
-        def _():
-            halo(k, side, piece).start()
-
-    def wait_halo(k):
-        for side in SIDES:
-            for piece in range(pieces if k == 1 else 1):
-                @pl.when(has[k][side])
-                def _(side=side, piece=piece):
-                    halo(k, side, piece).wait_send()
-
-                @pl.when(has[k][1 - side])
-                def _(side=side, piece=piece):
-                    halo(k, side, piece).wait_recv()
-
-    tile_lane = iota((16, SZ), 1)
-
-    def pack(packs, value, x):
-        value = pltpu.roll(value, (2 * x + 2) % SZ, 1)
-        low = tile_lane // 2 == (x + 1) % (SZ // 2)
-        return [jnp.where(low, value, packs[0]), jnp.where(tile_lane // 2 == x, value, packs[1])]
-
-    srows = s_v.reshape((SX + 4) * (SY + 16), SZ)
-    wrows, frows = w_v.reshape(SX * SY, SZ), f_v.reshape(SX * SY, SZ)
-
-    def sums(group):
-        for c in group:
-            for copy in loads[c]:
-                copy.wait()
-        for y in range(0, SY, 16):
-            rows = slice(y, y + 16)
-            packs = [zsend[0, rows], zsend[1, rows]]
-            for x in range(group[0] * SPF, (group[-1] + 1) * SPF):
-                s = w_v[x, rows] + f_v[x, rows]
-                s_v[x + 2, 8 + y:24 + y] = s
-                high, low = split2(s)
-                parts_v[x * SY + y:x * SY + y + 16, 0:SZ] = high
-                parts_v[x * SY + y:x * SY + y + 16, SZ:2 * SZ] = low
-                packs = pack(packs, s, x)
-            zsend[0, rows], zsend[1, rows] = packs
-
-    def yfaces(piece):
-        for side in SIDES:
-            for k in range(2):
-                y = k if side == 0 else SY - 2 + k
-                ysend[side, k, pl.ds(piece * each, each)] = srows[
-                    pl.ds((piece * each + 2) * (SY + 16) + 8 + y, each, stride=SY + 16), :]
-            start_halo(1, side, piece)
-
-    def forces(i, slot):
-        slopes = dot(parts_v[i * KV:(i + 1) * KV], band_v[...])
-        for y in range(0, SY, 16):
-            rows = slice(8 + y, 24 + y)
-            slabs = [s_v[i * SPF + x, rows] for x in range(SPF + 4)]
-            packs = [dz_v[0, y:y + 16], dz_v[1, y:y + 16]]
-            for xx in range(SPF):
-                x = i * SPF + xx
-                d = w_v[x, y:y + 16] - f_v[x, y:y + 16]
-                packs = pack(packs, d, x)
-                gx = slabs[xx] - slabs[xx + 4] + 8.0 * (slabs[xx + 3] - slabs[xx + 1])
-                gy = (s_v[x + 2, 6 + y:22 + y] - s_v[x + 2, 10 + y:26 + y]
-                      + 8.0 * (s_v[x + 2, 9 + y:25 + y] - s_v[x + 2, 7 + y:23 + y]))
-                gz = slopes[xx * SY + y:xx * SY + y + 16]
-                for a, g in enumerate((gx, gy, gz)):
-                    at = (slot, slice(xx * SY + y, xx * SY + y + 16),
-                          slice(a * SZ, (a + 1) * SZ))
-                    fh_v[at], fl_v[at] = split2(g * d)
-            dz_v[0, y:y + 16], dz_v[1, y:y + 16] = packs
-
-    lane = iota((SY, SZ), 1)
-
-    def gather(i, slot):
-        k, ph = divmod(i, per)
-        many = 5 * QE + 4 * QC
-        weights = jnp.concatenate([wf_v[0], wc_v[ph, 0], wf_v[1], wc_v[ph, 1]], axis=0)
-        both = dot(weights, fh_v[slot])
-        out = both[:many] + both[many:] + dot(weights[:many], fl_v[slot])
-        accf[i:i + 5] += out[:5 * QE].reshape(5, QE, lanes)
-        at = k + (1 if ph >= per // 2 else 0)
-        accc[:, at:at + 4] += out[5 * QE:].reshape(QC, 4, lanes)
-
-    def run_sums(group):
-        sums(group)
-        summed.append(group)
-
-    def run_faces():
-        while summed:
-            yfaces(summed.pop(0)[0] * SPF // each)
-
-    summed = []
-    for group in groups[:BEFORE]:
-        run_sums(group)
-    pl.semaphore_wait(barrier, total)
-    for d in range(1, nz):
-        pl.semaphore_signal(
-            in_sem, inc=1, device_id={"gz": lax.rem(me[2] + d, nz)}, device_id_type=MESH)
-    start_halo(0, 0)
-    start_halo(0, 1)
-    run_faces()
-    for group in groups[BEFORE:]:
-        run_sums(group)
-        run_faces()
-    start_halo(2, 0)
-    start_halo(2, 1)
-
     turn = list(range(1, cells - 1)) + [0, cells - 1]
     forces(turn[0], 0)
     for n, i in enumerate(turn):
@@ -425,7 +427,7 @@
         for k in range(2):
             y = k if side == 0 else SY - 2 + k
             at = pl.ds(y, SX, stride=SY)
-            adds.append(g[k] * (wrows[at, :] - frows[at, :]))
+            adds.append(g[k] * drows[at, :])
     high, low = split2(jnp.concatenate(adds, 0))
     weights = wy_v[0]
     added = dot(weights, high) + dot(wy_v[1], high) + dot(weights, low)

time: 19.5 us -> 18.8 us (0.964)
  Pallas kernels: 18.7 us -> 18.1 us
    pallas_call x1, Pallas kernels: 18 us -> 17.4 us  [step(): pl.pallas_call(functools.partial(kernel, sizes), out_shape=(pltpu.VMEM(fi...]
where the time goes in v5:
time: 18.8 us; the launch traced here: 18.7 us
  Pallas kernels  18.1 us (96%)
  between operations  0.64 us (3%)
    pallas_call x1, Pallas kernels, step(): pl.pallas_call(functools.partial(kernel, sizes), out_shape=(pltpu.VMEM(fi...  17.4 us
    pallas_call x1, Pallas kernels, step(): pl.pallas_call(write_out, out_shape=(jax.ShapeDtypeStruct(fine.shape, f32...  0.67 us

profile of v5, /device:TPU:0, one launch (start us, length us, event | category | flops | bytes accessed | tf_op | source)
XLA Modules:
  0.0 18.7 jit_solution(6867436333412641651)
XLA Ops:
  0.6 17.4 %shard_map.59 = (f32[3,8,8,16]{3,2,1,0:T(8,128)S(1)}, f32[3,32,128]{2,1,0:T(8,128)S(1)}) custom-call(f32[64,64,128]{2,1,0:T(8,128)} %w_hbm.1, f32[64,64,128]{2,1,0:T(8,128)} %f_hbm.1, f32[3,8,8,16]{3,2,1,0:T(8,128)} %fc_hbm.1, f32[3,8,4,16]{3,2,1,0:T(4,128)} %cc_hbm.1), custom_call_target="tpu_custom_call" | custom-call | tf_op jit(solution)/shard_map/pallas_call | solution.py:637
  18.0 0.7 %shard_map.60 = (f32[3,8,8,16]{3,2,1,0:T(8,128)}, f32[3,8,4,16]{3,2,1,0:T(4,128)}) custom-call(f32[3,8,8,16]{3,2,1,0:T(8,128)S(1)} %get-tuple-element.4.f_ref, f32[3,32,128]{2,1,0:T(8,128)S(1)} %get-tuple-element.5.c_ref), custom_call_target="tpu_custom_call" | custom-call | tf_op jit(solution)/shard_map/pallas_call | solution.py:671

commit v6 on v5

--- a/solution.py
+++ b/solution.py
@@ -46,6 +46,10 @@
 def split2(value):
     high = value.astype(bf16)
     return high, (value - high.astype(f32)).astype(bf16)
+
+
+def thrice(a, b):
+    return dot(a[0], b[0]) + dot(a[1], b[0]) + dot(a[0], b[1])
 
 
 def split3(value):
@@ -323,7 +327,7 @@
     rows, cols = iota((QC, SY), 0), iota((QC, SY), 1)
     put(wq_v, (slice(QE, QE + QC),), weight(cols + me[1] * SY, rows, SPC))
     col = iota((EX, KP), 1)
-    xat = jnp.where(col < SZ, (col + SZ - 2) % SZ, col % SZ) // 2
+    xat = jnp.where(col < SZ, col, (col - 2) % SZ) // 2
     wx_v[0:EX] = weight(xat, iota((EX, KP), 0) - 2, SPF)
     wx_v[EX:EX + XR] = weight(xat[0:XR], iota((XR, KP), 0) - 2, SPC)
 
@@ -414,9 +418,13 @@
     table = jnp.concatenate(
         [accf[2:2 + PX].reshape(PX * QE, lanes), accf[0:2].reshape(2 * QE, lanes),
          accf[2 + PX:].reshape(2 * QE, lanes), accc[...].reshape(NC, lanes)], 0)
-    high, low = split2(table)
-    whole_v[...] = dot(high, wz_v[0]) + dot(high, wz_v[1]) + dot(low, wz_v[0])
-    whole_v[0:NF, 0:LW] = whole_v[0:NF, 0:LW] + bend_v[...].reshape(NF, LW)
+    parts = split2(table)
+    both = ((slice(0, NF), slice(0, LW)), (slice(NF, NF + NC), slice(LW, 2 * LW)))
+    for rows, cols in both:
+        whole_v[rows] = thrice((parts[0][rows], parts[1][rows]),
+                               (wz_v[0, :, cols], wz_v[1, :, cols]))
+    whole_v[0:NF] = whole_v[0:NF] + bend_v[...].reshape(NF, LW)
+    dlow, dhigh = pltpu.roll(dz_v[0], SZ - 2, 1), pltpu.roll(dz_v[1], 2, 1)
 
     wait_halo(1)
     wait_halo(2)
@@ -428,27 +436,22 @@
             y = k if side == 0 else SY - 2 + k
             at = pl.ds(y, SX, stride=SY)
             adds.append(g[k] * drows[at, :])
-    high, low = split2(jnp.concatenate(adds, 0))
-    weights = wy_v[0]
-    added = dot(weights, high) + dot(wy_v[1], high) + dot(weights, low)
-
+    faces = split2(jnp.concatenate(adds, 0))
     even = lane % 2 == 0
     hl, hh = zrecv[0], zrecv[1]
     cl = jnp.where(even, hl - 8.0 * pltpu.roll(hl, SZ - 1, 1), hl)
     ch = jnp.where(even, -hh, 8.0 * pltpu.roll(hh, 1, 1) - hh)
-    fz = jnp.concatenate([pltpu.roll(cl, 2, 1) * dz_v[0],
-                          pltpu.roll(ch, SZ - 2, 1) * dz_v[1]], 1)
-    high, low = split2(fz)
-    g = dot(wq_v[0], high) + dot(wq_v[1], high) + dot(wq_v[0], low)
-    blocks = [g[0:QE] * wx_v[p:p + 1] for p in turned]
-    blocks += [g[QE + q:QE + q + 1] * wx_v[EX:EX + XR] for q in range(QC)]
-    hhigh, hlow = split2(jnp.concatenate(blocks, 0))
-
-    high, low = split2(added)
-    part = slice(SZ, 2 * SZ)
-    whole = whole_v[...] + (
-        dot(high, wz_v[0, part]) + dot(high, wz_v[1, part]) + dot(low, wz_v[0, part])
-        + dot(hhigh, wh_v[0]) + dot(hhigh, wh_v[1]) + dot(hlow, wh_v[0]))
+    g = thrice(wq_v, split2(jnp.concatenate([cl * dlow, ch * dhigh], 1)))
+
+    def with_halos(rows, cols, blocks):
+        added = thrice((wy_v[0, rows], wy_v[1, rows]), faces)
+        part = slice(SZ, 2 * SZ)
+        return whole_v[rows] + (
+            thrice(split2(added), (wz_v[0, part, cols], wz_v[1, part, cols]))
+            + thrice(split2(jnp.concatenate(blocks, 0)), (wh_v[0, :, cols], wh_v[1, :, cols])))
+
+    coarse = with_halos(
+        *both[1], [g[QE + q:QE + q + 1] * wx_v[EX:EX + XR] for q in range(QC)])
 
     pl.semaphore_wait(in_sem, nz - 1)
 
@@ -471,13 +474,16 @@
     for v in range(0, QC, PG):
         share = 0.0
         for q in range(v, min(v + PG, QC)):
-            tile = whole[NF + q * XR:NF + (q + 1) * XR, LW:2 * LW]
+            tile = coarse[q * XR:(q + 1) * XR]
             share = share + (tile if q == v else pltpu.roll(tile, (q - v) * GL, 1))
         all_v[mine, v // PG] = share[0:XC]
-    for o in far:
-        coarse_copy(o, mine).start()
-
-    fine = whole[0:NF, 0:LW]
+
+    @pl.when(me[0] >= 0)
+    def _():
+        for o in far:
+            coarse_copy(o, mine).start()
+
+    fine = with_halos(*both[0], [g[0:QE] * wx_v[p:p + 1] for p in turned])
     tall = jnp.concatenate([fine, jnp.zeros((2 * LW - NF, LW), f32)], 0).T
     fine = fine.reshape(EX, QE, LW)
     for side in SIDES:
@@ -652,7 +658,7 @@
                 V((2, KV, 3 * SZ), bf16), V((2, KV, 3 * SZ), bf16),
                 V((SX * SY, 2 * SZ), bf16), V((2 * SZ, SZ), bf16),
                 V((EX, QE, 3 * SZ), f32), V((QC, XR, 3 * SZ), f32),
-                V((NF + NC, 2 * LW), f32),
+                V((NF + NC, LW), f32),
                 V((PX + 6, PY + 16, LW), f32), V((PX + 6, PY + 16, LW), f32),
                 V((EX, QE, LW), f32),
                 V((KX + 2, KY + 16, LW), f32), V((KX + 2, KY + 16, LW), f32),

time: 18.8 us -> 18.3 us (0.973)
  Pallas kernels: 18.1 us -> 17.6 us
    pallas_call x1, Pallas kernels: 17.4 us -> 16.9 us  [step(): pl.pallas_call(functools.partial(kernel, sizes), out_shape=(pltpu.VMEM(fi...]
where the time goes in v6:
time: 18.3 us; the launch traced here: 18.2 us
  Pallas kernels  17.6 us (96%)
  between operations  0.64 us (3%)
    pallas_call x1, Pallas kernels, step(): pl.pallas_call(functools.partial(kernel, sizes), out_shape=(pltpu.VMEM(fi...  16.9 us
    pallas_call x1, Pallas kernels, step(): pl.pallas_call(write_out, out_shape=(jax.ShapeDtypeStruct(fine.shape, f32...  0.67 us

profile of v6, /device:TPU:0, one launch (start us, length us, event | category | flops | bytes accessed | tf_op | source)
XLA Modules:
  0.0 18.2 jit_solution(15093284963384950519)
XLA Ops:
  0.6 16.9 %shard_map.59 = (f32[3,8,8,16]{3,2,1,0:T(8,128)S(1)}, f32[3,32,128]{2,1,0:T(8,128)S(1)}) custom-call(f32[64,64,128]{2,1,0:T(8,128)} %w_hbm.1, f32[64,64,128]{2,1,0:T(8,128)} %f_hbm.1, f32[3,8,8,16]{3,2,1,0:T(8,128)} %fc_hbm.1, f32[3,8,4,16]{3,2,1,0:T(4,128)} %cc_hbm.1), custom_call_target="tpu_custom_call" | custom-call | tf_op jit(solution)/shard_map/pallas_call | solution.py:643
  17.5 0.7 %shard_map.60 = (f32[3,8,8,16]{3,2,1,0:T(8,128)}, f32[3,8,4,16]{3,2,1,0:T(4,128)}) custom-call(f32[3,8,8,16]{3,2,1,0:T(8,128)S(1)} %get-tuple-element.4.f_ref, f32[3,32,128]{2,1,0:T(8,128)S(1)} %get-tuple-element.5.c_ref), custom_call_target="tpu_custom_call" | custom-call | tf_op jit(solution)/shard_map/pallas_call | solution.py:677

commit v7 on v6

--- a/solution.py
+++ b/solution.py
@@ -115,17 +115,16 @@
     for copy in small:
         copy.start()
     loads = []
-    for c in range(cells):
-        part = pl.ds(c * SPF, SPF)
-        loads.append((
-            pltpu.make_async_copy(w_hbm.at[part], w_v.at[part], load_sem.at[0, c]),
-            pltpu.make_async_copy(f_hbm.at[part], f_v.at[part], load_sem.at[1, c]),
-        ))
     groups = [(0, 1), (cells - 2, cells - 1)]
     groups += [(c, c + 1) for c in range(2, cells - 2, 2)]
-    for c in sum(groups, ()):
-        loads[c][0].start()
-        loads[c][1].start()
+    for n, group in enumerate(groups):
+        part = pl.ds(group[0] * SPF, len(group) * SPF)
+        loads.append((
+            pltpu.make_async_copy(w_hbm.at[part], w_v.at[part], load_sem.at[0, n]),
+            pltpu.make_async_copy(f_hbm.at[part], f_v.at[part], load_sem.at[1, n]),
+        ))
+        for copy in loads[n]:
+            copy.start()
 
     for at in (0, SX + 2):
         s_v[at:at + 2, 8:8 + SY, :] = jnp.zeros((2, SY, SZ), f32)
@@ -226,9 +225,8 @@
     drows = w_v.reshape(SX * SY, SZ)
 
     def sums(group):
-        for c in group:
-            for copy in loads[c]:
-                copy.wait()
+        for copy in loads[groups.index(group)]:
+            copy.wait()
         for y in range(0, SY, 16):
             rows = slice(y, y + 16)
             packs = [zsend[0, rows], zsend[1, rows]]
@@ -505,7 +503,7 @@
             src, dst = ym_v.at[pl.ds(0, PX)], yg_v.at[ys]
         else:
             src, dst = ym_v.at[pl.ds(PX if dx < 0 else PX + 2, 2)], cg_v.at[xs, ys]
-        at = (dx + 1, dy + 1, dz + 1)
+        at = (dx + 1, dy + 1 if ny > 2 else abs(dy), dz + 1)
         return pltpu.make_async_remote_copy(
             src_ref=src, dst_ref=dst, send_sem=as_sem.at[at], recv_sem=ar_sem.at[at],
             device_id=(me[0] + dx, me[1] + dy, me[2] + dz), device_id_type=MESH)
@@ -666,8 +664,8 @@
                 V((2, 2, PY, LW), f32), V((EX, 4, LW), f32),
                 V((2, 2, PY, LW), f32), V((2, PX, 4, LW), f32), V((2, 2, 2, 4, LW), f32),
                 V((nx * ny * nz, -(-QC // 4), SX // SPC + 4, LW), f32),
-                D((2, SX // SPF)), D((2,)), D((3, 2)), D((3, 2)), D((2, 4)), D((2, 4)),
-                D((3, 3, 3)), D((3, 3, 3)), D(()), D(()), pltpu.SemaphoreType.REGULAR,
+                D((2, SX // SPF // 2)), D((2,)), D((3, 2)), D((3, 2)), D((2, 4)), D((2, 4)),
+                D((3, 3 if ny > 2 else 2, 3)), D((3, 3 if ny > 2 else 2, 3)), D(()), D(()), pltpu.SemaphoreType.REGULAR,
             ],
             compiler_params=pltpu.CompilerParams(
                 collective_id=0, has_side_effects=True, vmem_limit_bytes=64000000

time: 18.3 us -> 18.1 us (0.989)
  Pallas kernels: 17.6 us -> 17.3 us
    pallas_call x1, Pallas kernels: 16.9 us -> 16.7 us  [step(): pl.pallas_call(functools.partial(kernel, sizes), out_shape=(pltpu.VMEM(fi...]
where the time goes in v7:
time: 18.1 us; the launch traced here: 18 us
  Pallas kernels  17.3 us (96%)
  between operations  0.64 us (4%)
    pallas_call x1, Pallas kernels, step(): pl.pallas_call(functools.partial(kernel, sizes), out_shape=(pltpu.VMEM(fi...  16.7 us
    pallas_call x1, Pallas kernels, step(): pl.pallas_call(write_out, out_shape=(jax.ShapeDtypeStruct(fine.shape, f32...  0.67 us

profile of v7, /device:TPU:0, one launch (start us, length us, event | category | flops | bytes accessed | tf_op | source)
XLA Modules:
  0.0 18.0 jit_solution(9501947270439281313)
XLA Ops:
  0.6 16.7 %shard_map.59 = (f32[3,8,8,16]{3,2,1,0:T(8,128)S(1)}, f32[3,32,128]{2,1,0:T(8,128)S(1)}) custom-call(f32[64,64,128]{2,1,0:T(8,128)} %w_hbm.1, f32[64,64,128]{2,1,0:T(8,128)} %f_hbm.1, f32[3,8,8,16]{3,2,1,0:T(8,128)} %fc_hbm.1, f32[3,8,4,16]{3,2,1,0:T(4,128)} %cc_hbm.1), custom_call_target="tpu_custom_call" | custom-call | tf_op jit(solution)/shard_map/pallas_call | solution.py:641
  17.3 0.7 %shard_map.60 = (f32[3,8,8,16]{3,2,1,0:T(8,128)}, f32[3,8,4,16]{3,2,1,0:T(4,128)}) custom-call(f32[3,8,8,16]{3,2,1,0:T(8,128)S(1)} %get-tuple-element.4.f_ref, f32[3,32,128]{2,1,0:T(8,128)S(1)} %get-tuple-element.5.c_ref), custom_call_target="tpu_custom_call" | custom-call | tf_op jit(solution)/shard_map/pallas_call | solution.py:675
